TPU v7x, 32 devices: a whole 2x2x4 slice. The times are simulated.
32 devices in a mesh: ka: 16 (over z, y, core), ga: 2 (over x).
Axes of the slice: x: 2, y: 2, z: 4, core: 2. Of those that a mesh axis runs over, the one named last changes fastest.
Arguments:
- coeffs: bfloat16 [16, 240, 2, 64, 128], P('ka', 'ga'), may hold values from -0.44921875 to 0.44921875
- neighbour: int32 [16, 3], P('ka'), may hold values from 0 to 15, as said below
- shift_id: int32 [16, 3], P('ka'), may hold values from 0 to 7
- block_map: int32 [8, 240], replicated, may hold values from 0 to 239, as said below
Outputs:
- intersection: float32 [16, 3, 2, 64, 64], P('ka', None, None, 'ga')
Inputs may be any that keep to these rules, and one draw needn't show every extreme that they name: `neighbour`: the k-points are numbered helically. The three columns of row k hold (k + 1) mod 16, (k + 4) mod 16 and (k + 8) mod 16, in an order drawn for each row. `block_map`: each row is a permutation of the 240 blocks. Block j lies in G-slice j // 120. In every row, each G-slice receives exactly 20 of its blocks from one other G-slice, exactly 10 from each of the remaining other G-slices, and the rest from itself.
All inputs are finite; a program needn't handle non-finite values.
Results may differ from a plain program's by a relative error of at most 0.0003.
Values may be sent and summed in bfloat16 or wider, within the bound.
A program may use at most 128 MiB of HBM per device.

v0:
```python
import functools

import jax
import jax.numpy as jnp
from jax import lax
from jax.sharding import PartitionSpec as P
from jax.experimental import pallas as pl
from jax.experimental.pallas import tpu as pltpu

CHUNKS = 4


def shifted(block, axis, distance):
    devices = range(lax.axis_size(axis))
    route = [((i - distance) % len(devices), i) for i in devices]
    return lax.ppermute(block, axis, route)


def complex_intersection(bra_real, bra_imag, ket_real, ket_imag, form):
    real_part = jnp.einsum(form, bra_real, ket_real, preferred_element_type=jnp.float32)
    real_part = real_part + jnp.einsum(form, bra_imag, ket_imag, preferred_element_type=jnp.float32)
    imag_part = jnp.einsum(form, bra_real, ket_imag, preferred_element_type=jnp.float32)
    imag_part = imag_part - jnp.einsum(form, bra_imag, ket_real, preferred_element_type=jnp.float32)
    return jnp.stack([real_part, imag_part], axis=-3)


def slot_plan(
    home_slice, target_slice, sent_local, place_local, my_slice, slices, capacity, slab_blocks
):
    targets = jnp.arange(slices, dtype=jnp.int32)
    chosen = (home_slice == my_slice)[:, None, :] & (
        target_slice[:, None, :] == targets[None, :, None]
    )
    chosen = chosen & (targets != my_slice)[None, :, None]
    counted = jnp.cumsum(chosen.astype(jnp.int32), axis=2) - 1
    places = jnp.arange(capacity, dtype=jnp.int32)
    matched = (
        chosen[:, :, None, :] & (counted[:, :, None, :] == places[None, None, :, None])
    ).astype(jnp.int32)
    filled = jnp.sum(matched, axis=3)
    sent_block = jnp.sum(matched * sent_local[:, None, None, :], axis=3)
    where_to = jnp.sum(matched * place_local[:, None, None, :], axis=3) + (1 - filled) * slab_blocks
    pair_count = home_slice.shape[0]
    return (
        sent_block.reshape(pair_count, slices * capacity),
        where_to.reshape(pair_count, slices * capacity),
    )


def on_device(coeffs, neighbour, shift_id, block_map):
    k_local = coeffs.shape[0]
    slab_blocks = coeffs.shape[1]
    band_count = coeffs.shape[3]
    lane_width = coeffs.shape[4]
    vector_count = neighbour.shape[1]
    cycle_size = lax.axis_size("ka")
    slices = lax.axis_size("ga")
    my_cycle = lax.axis_index("ka")
    my_slice = lax.axis_index("ga")
    capacity = 2 * max(1, slab_blocks // 12)
    all_blocks = slab_blocks * slices
    pair_count = k_local * vector_count
    k_total = k_local * cycle_size
    row_points = min(16, k_total // 4)
    row_devices = row_points // k_local
    pad_spec = ((0, 0), (0, 1), (0, 0), (0, 0), (0, 0))
    row_point = shifted(coeffs, "ka", -1)
    row_source = jnp.mod(my_cycle + 1, cycle_size)
    plane_kets = shifted(coeffs, "ka", -row_devices)
    plane_source = jnp.mod(my_cycle + row_devices, cycle_size)
    opposite = shifted(coeffs, "ka", cycle_size // 2)
    targets_flat = neighbour.reshape(-1)
    shifts_flat = shift_id.reshape(-1)
    target_device = targets_flat // k_local
    target_lane = targets_flat - target_device * k_local
    ket_index = jnp.where(
        target_device == my_cycle,
        target_lane,
        jnp.where(
            target_device == row_source,
            k_local,
            jnp.where(
                target_device == plane_source,
                k_local + 1 + target_lane,
                2 * k_local + 1 + target_lane,
            ),
        ),
    )
    bra_index = jnp.arange(pair_count, dtype=jnp.int32) // vector_count
    picks = (
        shifts_flat[:, None] == jnp.arange(block_map.shape[0], dtype=jnp.int32)[None, :]
    ).astype(jnp.int32)
    relabel = jnp.sum(picks[:, :, None] * block_map[None, :, :], axis=1)
    dest_global = jnp.broadcast_to(jnp.arange(all_blocks, dtype=jnp.int32)[None, :], relabel.shape)
    source_slice = relabel // slab_blocks
    dest_slice = dest_global // slab_blocks
    source_local = relabel - source_slice * slab_blocks
    dest_local = dest_global - dest_slice * slab_blocks
    kets = jnp.pad(jnp.concatenate([coeffs, row_point, plane_kets, opposite], axis=0), pad_spec)
    own_source = lax.dynamic_slice_in_dim(relabel, my_slice * slab_blocks, slab_blocks, 1)
    self_place = jnp.where(
        own_source // slab_blocks == my_slice, own_source - my_slice * slab_blocks, slab_blocks
    )
    ket_self = kets[ket_index[:, None], self_place]
    ket_self = ket_self.reshape(k_local, vector_count, slab_blocks, 2, band_count, lane_width)
    local_terms = complex_intersection(
        coeffs[:, :, 0],
        coeffs[:, :, 1],
        ket_self[:, :, :, 0],
        ket_self[:, :, :, 1],
        "ksmw,kbsnw->kbmn",
    )
    sent_block, where_to = slot_plan(
        dest_slice, source_slice, dest_local, source_local, my_slice, slices, capacity, slab_blocks
    )
    payload = coeffs[bra_index[:, None], sent_block]
    owner = jnp.broadcast_to(ket_index[:, None], (pair_count, slices))
    blocks = lax.all_to_all(payload, "ga", split_axis=1, concat_axis=1, tiled=True)
    places_in = lax.all_to_all(where_to, "ga", split_axis=1, concat_axis=1, tiled=True)
    owners = lax.all_to_all(owner, "ga", split_axis=1, concat_axis=1, tiled=True)
    partner = kets[owners[:, 0][:, None], places_in]
    remote = complex_intersection(
        blocks[:, :, 0], blocks[:, :, 1], partner[:, :, 0], partner[:, :, 1], "ismw,isnw->imn"
    )
    summed_part = local_terms + remote.reshape(k_local, vector_count, 2, band_count, band_count)
    total = lax.psum(summed_part, "ga")
    row_count = band_count // slices
    return lax.dynamic_slice_in_dim(total, my_slice * row_count, row_count, 3)


def gather_kernel(count, index_ref, source_ref, out_ref, sems):
    def copy(i):
        return pltpu.make_async_copy(source_ref.at[index_ref[i]], out_ref.at[i], sems.at[i])

    def begin(i, carry):
        copy(i).start()
        return carry

    def finish(i, carry):
        copy(i).wait()
        return carry

    lax.fori_loop(0, count, begin, 0)
    lax.fori_loop(0, count, finish, 0)


def gather_blocks(index, source):
    count = index.shape[0]
    shape = (count,) + source.shape[1:]
    return pl.pallas_call(
        functools.partial(gather_kernel, count),
        out_shape=jax.ShapeDtypeStruct(shape, source.dtype),
        in_specs=[
            pl.BlockSpec(memory_space=pltpu.SMEM),
            pl.BlockSpec(memory_space=pl.ANY),
        ],
        out_specs=pl.BlockSpec(memory_space=pltpu.VMEM),
        scratch_shapes=[pltpu.SemaphoreType.DMA((count,))],
        name="gather_blocks",
        cost_estimate=pl.CostEstimate(flops=0, bytes_accessed=4 * source.dtype.itemsize * count * source[0].size, transcendentals=0),
    )(index, source)


def plan_kernel(slab, capacity, shift_ref, map_ref, local_ref, sent_ref, got_ref):
    mine = lax.axis_index("ga")
    base = mine * slab
    for e in range(4):
        shift = shift_ref[e]

        def here(j, counts):
            own, out = counts
            source = map_ref[shift, base + j] - base
            inside = (source >= 0) & (source < slab)
            local_ref[0, e, own] = j
            local_ref[1, e, own] = source
            sent_ref[e, out] = j
            return own + inside.astype(jnp.int32), out + 1 - inside.astype(jnp.int32)

        def there(j, count):
            source = map_ref[shift, slab - base + j] - base
            inside = (source >= 0) & (source < slab)
            got_ref[e, count] = source
            return count + inside.astype(jnp.int32)

        lax.fori_loop(0, slab, here, (jnp.int32(0), jnp.int32(0)), unroll=8)
        lax.fori_loop(0, slab, there, jnp.int32(0), unroll=8)


def plan(shifts, block_map, slab, capacity):
    own_count = slab - capacity
    return pl.pallas_call(
        functools.partial(plan_kernel, slab, capacity),
        out_shape=(
            jax.ShapeDtypeStruct((2, 4, own_count + 8), jnp.int32),
            jax.ShapeDtypeStruct((4, capacity + 8), jnp.int32),
            jax.ShapeDtypeStruct((4, capacity + 8), jnp.int32),
        ),
        in_specs=[pl.BlockSpec(memory_space=pltpu.SMEM)] * 2,
        out_specs=[pl.BlockSpec(memory_space=pltpu.SMEM)] * 3,
        name="plan",
    )(shifts, block_map)


def meet_kernel(
    points, slab, capacity, local_ref, other_ref, send_ref, own_hbm, mine_out, out_ref,
    own, upper, lower, nxt, got_own, lower_out, got_lower, local_sems, send_sems, recv_sems,
):
    row = points // 4
    me = lax.axis_index("ka")
    partner = 1 - lax.axis_index("ga")
    z, column = me // row, me % row
    even = column % 2 == 0
    middle = (z == 1) | (z == 2)
    holds_pair = middle
    below = {"ka": (me + points - row) % points}
    above = {"ka": (me + row) % points}
    left = {"ka": z * row + (column + row - 1) % row}
    right = {"ka": z * row + (column + 1) % row}
    across = {"ga": partner}
    bands, lanes = own.shape[2], own.shape[3]
    size = slab // CHUNKS
    own_count = slab - capacity

    barrier = pltpu.get_barrier_semaphore()
    for peer in (below, above, left, right, across):
        pl.semaphore_signal(barrier, inc=1, device_id=peer, device_id_type=pl.DeviceIdType.MESH)
    pl.semaphore_wait(barrier, 5)

    def remote(source, target, n, peer):
        return pltpu.make_async_remote_copy(
            src_ref=source, dst_ref=target, send_sem=send_sems.at[n], recv_sem=recv_sems.at[n],
            device_id=peer, device_id_type=pl.DeviceIdType.MESH,
        )

    def chunk(c):
        return pl.ds(c * size, size)

    keep = pltpu.make_async_copy(own_hbm, own, local_sems.at[0])
    swap_own = remote(mine_out, got_own, 0, across)
    swap_lower = remote(lower_out, got_lower, 1, across)
    rise = [remote(own_hbm.at[chunk(c)], lower.at[chunk(c)], 2 + c, above) for c in range(CHUNKS)]
    fall = [remote(own_hbm.at[chunk(c)], upper.at[chunk(c)], 2 + CHUNKS + c, below) for c in range(CHUNKS)]
    pass_own = [remote(own_hbm.at[chunk(c)], nxt.at[chunk(c)], 2 + 2 * CHUNKS + c, left) for c in range(CHUNKS)]
    pass_on = [remote(upper.at[chunk(c)], nxt.at[chunk(c)], 2 + 2 * CHUNKS + c, left) for c in range(CHUNKS)]

    falls = even | (z >= 2)
    rises = ~even | (z <= 1)
    gets_upper = even | middle
    gets_lower = ~even | middle

    keep.start()
    swap_own.start()
    for c in range(CHUNKS):

        @pl.when(even & rises)
        def _():
            rise[c].start()

        @pl.when(~even & falls)
        def _():
            fall[c].start()

    for c in range(CHUNKS):

        @pl.when(column > 0)
        def _():
            pass_own[c].start()

        @pl.when(even)
        def _():
            fall[c].start()

        @pl.when(~even)
        def _():
            rise[c].start()

    def pick(ref, at):
        return ref[at].reshape(2 * bands, lanes)

    def product(total, first_left, second_left, first_right, second_right):
        return total + lax.dot_general(
            jnp.concatenate([first_left, second_left], axis=1),
            jnp.concatenate([first_right, second_right], axis=1),
            (((1,), (1,)), ((), ())),
            preferred_element_type=jnp.float32,
        )

    def edge(e, bra, ket, got, got_at, bra_sent):
        def own_step(i, total):
            for u in range(0, 10, 2):
                n = i * 10 + u
                total = product(
                    total,
                    pick(bra, local_ref[0, e, n]), pick(bra, local_ref[0, e, n + 1]),
                    pick(ket, local_ref[1, e, n]), pick(ket, local_ref[1, e, n + 1]),
                )
            return total

        def cross_step(i, total):
            n = i * 2
            travelled = pick(got, got_at + n), pick(got, got_at + n + 1)
            stayed_ref = ket if bra_sent else bra
            stayed = pick(stayed_ref, other_ref[e, n]), pick(stayed_ref, other_ref[e, n + 1])
            if bra_sent:
                return product(total, *travelled, *stayed)
            return product(total, *stayed, *travelled)

        total = jnp.zeros((2 * bands, 2 * bands), jnp.float32)
        total = lax.fori_loop(0, own_count // 10, own_step, total)
        total = lax.fori_loop(0, capacity // 2, cross_step, total)
        out_ref[e, 0] = total[:bands, :bands] + total[bands:, bands:]
        out_ref[e, 1] = total[:bands, bands:] - total[bands:, :bands]

    keep.wait()
    swap_own.wait_recv()

    def next_edge():
        for copy in pass_own:
            copy.wait_recv()
        edge(0, own, nxt, got_own, 0, True)

    @pl.when(column < row - 1)
    def _():
        next_edge()

    @pl.when(gets_upper)
    def _():
        for copy, onward in zip(fall, pass_on):
            copy.wait_recv()

            @pl.when(column == 0)
            def _():
                onward.start()

    @pl.when(gets_lower)
    def _():
        for copy in rise:
            copy.wait_recv()

    @pl.when(holds_pair)
    def _():
        def gather(r, carry):
            lower_out[r] = lower[send_ref[r]]
            return carry

        lax.fori_loop(0, 2 * capacity, gather, 0)
        swap_lower.start()

    @pl.when(even)
    def _():
        edge(1, own, upper, got_own, capacity, True)

    @pl.when(~even)
    def _():
        edge(1, lower, own, got_own, capacity, False)

    @pl.when(column == row - 1)
    def _():
        next_edge()

    @pl.when(holds_pair)
    def _():
        swap_lower.wait_recv()
        edge(2, lower, upper, got_lower, 0, True)
        edge(3, upper, lower, got_lower, capacity, False)
        swap_lower.wait_send()

    @pl.when(~holds_pair)
    def _():
        out_ref[2] = jnp.zeros_like(out_ref[2])
        out_ref[3] = jnp.zeros_like(out_ref[3])

    swap_own.wait_send()

    @pl.when(falls)
    def _():
        for copy in fall:
            copy.wait_send()

    @pl.when(rises)
    def _():
        for copy in rise:
            copy.wait_send()

    @pl.when(column > 0)
    def _():
        for copy in pass_own:
            copy.wait_send()

    @pl.when(column == 0)
    def _():
        for copy in pass_on:
            copy.wait_send()


def meet(local, other, send, own, mine_out, points, capacity):
    slab, bands = own.shape[0], own.shape[2]
    block = own.shape[1:]
    copies = 2 + 3 * CHUNKS
    return pl.pallas_call(
        functools.partial(meet_kernel, points, slab, capacity),
        out_shape=jax.ShapeDtypeStruct((4, 2, bands, bands), jnp.float32),
        in_specs=[pl.BlockSpec(memory_space=pltpu.SMEM)] * 3 + [pl.BlockSpec(memory_space=pl.ANY)] * 2,
        out_specs=pl.BlockSpec(memory_space=pltpu.VMEM),
        scratch_shapes=[pltpu.VMEM((slab,) + block, own.dtype)] * 4
        + [pltpu.VMEM((2 * capacity,) + block, own.dtype)] * 3
        + [pltpu.SemaphoreType.DMA((1,)), pltpu.SemaphoreType.DMA((copies,)), pltpu.SemaphoreType.DMA((copies,))],
        compiler_params=pltpu.CompilerParams(
            collective_id=0, has_side_effects=True, vmem_limit_bytes=32 * 2**20
        ),
        name="meet",
    )(local, other, send, own, mine_out)


def on_four_rows(coeffs, neighbour, shift_id, block_map):
    own = coeffs[0]
    slab = own.shape[0]
    points = lax.axis_size("ka")
    row = points // 4
    me = lax.axis_index("ka")
    first = lax.axis_index("ga") == 0
    even = jnp.mod(jnp.mod(me, row), 2) == 0
    capacity = 2 * max(1, slab // 12)
    to_lower = [((k + row) % points, k) for k in range(points)]
    to_upper = [((k - row) % points, k) for k in range(points)]
    swap = [(0, 1), (1, 0)]

    def role_shift(step):
        return jnp.sum(jnp.where(neighbour[0] == jnp.mod(me + step, points), shift_id[0], 0))

    row_shift, half_shift = role_shift(row), role_shift(points // 2)
    sent = jnp.stack([row_shift, half_shift])
    lower = lax.ppermute(sent, "ka", to_upper)
    upper = lax.ppermute(sent, "ka", to_lower)
    shifts = jnp.stack([role_shift(1), jnp.where(even, row_shift, lower[0]), lower[1], upper[1]])

    local, bras, kets = plan(shifts, block_map, slab, capacity)
    bras, kets = bras[:, :capacity], kets[:, :capacity]
    sends_bra = jnp.stack([even | True, even, even | True, even & False])[:, None]
    send = jnp.where(sends_bra, bras, kets)
    other = jnp.where(sends_bra, kets, bras)
    mine_out = gather_blocks(send[:2].reshape(-1), own)
    sums = meet(local, other, send[2:].reshape(-1), own, mine_out, points, capacity)

    half = sums.shape[2] // 2
    low_rows, high_rows = sums[:, :, :half], sums[:, :, half:]
    kept = jnp.where(first, low_rows, high_rows)
    total = kept + lax.ppermute(jnp.where(first, high_rows, low_rows), "ga", swap)
    from_upper = lax.ppermute(total[1:3], "ka", to_lower)
    from_lower = lax.ppermute(total[3], "ka", to_upper)
    row_sum = jnp.where(even, total[1], from_upper[0])
    half_sum = from_upper[1] + from_lower
    target = neighbour[0][:, None, None, None]
    out = jnp.where(
        target == jnp.mod(me + 1, points),
        total[0],
        jnp.where(target == jnp.mod(me + row, points), row_sum, half_sum),
    )
    return out[None]


def solution(mesh):
    in_specs = (P("ka", "ga", None, None, None), P("ka", None), P("ka", None), P())
    out_specs = P("ka", None, None, "ga", None)
    four_rows = mesh.shape["ga"] == 2 and mesh.shape["ka"] == 4 * min(16, mesh.shape["ka"] // 4)

    def run(coeffs, neighbour, shift_id, block_map):
        one_each = coeffs.shape[0] == mesh.shape["ka"]
        per_slice = coeffs.shape[1] // mesh.shape["ga"]
        whole_chunks = per_slice % (2 * CHUNKS) == 0 or per_slice % CHUNKS == 0 and per_slice % 2 == 0
        body = on_four_rows if four_rows and one_each and whole_chunks else on_device
        return jax.shard_map(
            body, mesh=mesh, in_specs=in_specs, out_specs=out_specs, check_vma=False
        )(coeffs, neighbour, shift_id, block_map)

    return run
```

profile of v0, /device:TPU:5, one launch (start us, length us, event | category | flops | bytes accessed | tf_op | source)
XLA Modules:
  0.0 195.8 jit_solution(17366008245291745012)
XLA Ops:
  0.0 1.4 fusion.3
  1.4 1.3 pad_add_fusion.1
  2.7 3.3 %collective-permute-start.1 = (s32[2]{0:T(128)S(1)}, s32[2]{0:T(128)S(1)}, u32[]{:S(2)}, u32[]{:S(2)}) collective-permute-start(s32[2]{0:T(128)S(1)} %pad_add_fusion.1), channel_id=1, source_target_pairs={{8,0},{10,2},{12,4},{14,6},{16,8},{18,10},{20,12},{22,14},{24,16},... | collective-permute-start | bytes 32 | tf_op jit(solution)/shard_map/ppermute | solution.py:434
  6.1 0.0 collective-permute-start
  6.1 0.1 pad_add_fusion
  6.1 4.1 %collective-permute-done = s32[2]{0:T(128)S(1)} collective-permute-done((s32[2]{0:T(128)S(1)}, s32[2]{0:T(128)S(1)}, u32[]{:S(2)}, u32[]{:S(2)}) %collective-permute-start) | collective-permute-done | bytes 40 | tf_op jit(solution)/shard_map/ppermute | solution.py:433
  10.3 0.7 fusion.6
  12.2 0.0 collective-permute-done.1
  12.2 0.6 slice.47
  12.8 2.5 %pad_add_fusion.2.shift_ref = s32[4]{0:T(128)} fusion(s32[1]{0:T(128)} %slice.47, s32[1]{0:T(128)} %get-tuple-element.24, s32[1]{0:T(128)} %bitcast.8, s32[1]{0:T(128)} %bitcast.2), kind=kLoop, calls=%fused_computation.17 | loop fusion | flops 12 | bytes 32 | tf_op jit(solution)/shard_map/stack | solution.py:435
  15.3 8.9 %plan.1 = (s32[2,4,108]{2,1,0:T(4,128)}, s32[4,28]{1,0:T(4,128)}, s32[4,28]{1,0:T(4,128)}) custom-call(s32[4]{0:T(128)} %pad_add_fusion.2.shift_ref, s32[8,240]{1,0:T(8,128)} %map_ref.1), custom_call_target="tpu_custom_call" | custom-call | tf_op jit(solution)/shard_map/plan/pallas_call | solution.py:191
  24.2 0.0 copy-start.2
  24.2 0.8 slice_select_fusion.2
  25.0 0.7 reshape.36.index_ref
  25.7 0.1 reshape.35.send_ref
  25.8 3.4 %gather_blocks.1.mine_out = bf16[40,2,64,128]{3,2,1,0:T(8,128)(2,1)} custom-call(s32[40]{0:T(128)} %reshape.36.index_ref, bf16[120,2,64,128]{3,2,1,0:T(8,128)(2,1)} %bitcast.35), custom_call_target="tpu_custom_call" | custom-call | bytes 5242880 | tf_op jit(solution)/shard_map/gather_blocks/pallas_call | solution.py:150
  29.1 0.0 copy-done.2
  29.2 0.0 copy-start
  29.2 2.1 %copy-done = bf16[1,120,2,64,128]{4,3,2,1,0:T(8,128)(2,1)S(1)} copy-done((bf16[1,120,2,64,128]{4,3,2,1,0:T(8,128)(2,1)S(1)}, bf16[1,120,2,64,128]{4,3,2,1,0:T(8,128)(2,1)}, u32[]{:S(2)}) %copy-start) | copy-done | bytes 3932184
  31.3 0.0 copy-start.1
  31.3 1.3 copy-done.1
  32.6 140.7 %meet.1 = f32[4,2,64,64]{3,2,1,0:T(8,128)S(1)} custom-call(s32[2,4,108]{2,1,0:T(4,128)S(1)} %copy-done.2, s32[4,20]{1,0:T(4,128)S(1)} %get-tuple-element.20.other_ref, s32[40]{0:T(128)S(1)} %reshape.35.send_ref, bf16[120,2,64,128]{3,2,1,0:T(8,128)(2,1)S(1)} %bitcast.36, bf16[40,2,64,128]{3,2,1,0:T(8,128)(2,1)S(1)} %copy-done.1), custom_call_target="tpu_custom_call" | custom-call | tf_op jit(solution)/shard_map/meet/pallas_call | solution.py:400
  173.3 1.3 collective-permute-start.2
  174.6 2.6 %collective-permute-done.2 = f32[4,2,32,64]{3,2,1,0:T(8,128)S(1)} collective-permute-done((f32[4,2,32,64]{3,2,1,0:T(8,128)S(1)}, f32[4,2,32,64]{3,2,1,0:T(8,128)S(1)}, u32[]{:S(2)}, u32[]{:S(2)}) %collective-permute-start.2) | collective-permute-done | bytes 65568 | tf_op jit(solution)/shard_map/ppermute | solution.py:448
  177.2 11.5 %collective-permute-start.3 = (f32[2,2,32,64]{3,2,1,0:T(8,128)S(1)}, f32[2,2,32,64]{3,2,1,0:T(8,128)S(1)}, u32[]{:S(2)}, u32[]{:S(2)}) collective-permute-start(f32[2,2,32,64]{3,2,1,0:T(8,128)S(1)} %slice.62), channel_id=1, source_target_pairs={{8,0},{10,2},{12,4},{14,6},{16,8},{18,10},{20,12},{22,14},{24,16},... | collective-permute-start | bytes 98312 | tf_op jit(solution)/shard_map/ppermute | solution.py:449
  188.8 1.3 collective-permute-done.3
  190.1 0.1 collective-permute-start.4
  190.2 4.9 %collective-permute-done.4 = f32[2,32,64]{2,1,0:T(8,128)S(1)} collective-permute-done((f32[2,32,64]{2,1,0:T(8,128)S(1)}, f32[2,32,64]{2,1,0:T(8,128)S(1)}, u32[]{:S(2)}, u32[]{:S(2)}) %collective-permute-start.4) | collective-permute-done | bytes 16416 | tf_op jit(solution)/shard_map/ppermute | solution.py:450
  195.0 0.7 select_select_fusion
  (6 shorter events, 0.1 us)
Async XLA Ops:
  2.7 9.4 %collective-permute-start.1 = (s32[2]{0:T(128)S(1)}, s32[2]{0:T(128)S(1)}, u32[]{:S(2)}, u32[]{:S(2)}) collective-permute-start(s32[2]{0:T(128)S(1)} %pad_add_fusion.1), channel_id=1, source_target_pairs={{8,0},{10,2},{12,4},{14,6},{16,8},{18,10},{20,12},{22,14},{24,16},... | collective-permute-start | bytes 32 | tf_op jit(solution)/shard_map/ppermute | solution.py:434
  6.1 4.2 %collective-permute-start = (s32[2]{0:T(128)S(1)}, s32[2]{0:T(128)S(1)}, u32[]{:S(2)}, u32[]{:S(2)}) collective-permute-start(s32[2]{0:T(128)S(1)} %pad_add_fusion.1), channel_id=1, source_target_pairs={{24,0},{26,2},{28,4},{30,6},{0,8},{2,10},{4,12},{6,14},{8,16},{10,... | collective-permute-start | bytes 32 | tf_op jit(solution)/shard_map/ppermute | solution.py:433
  24.2 4.9 %copy-start.2 = (s32[2,4,108]{2,1,0:T(4,128)S(1)}, s32[2,4,108]{2,1,0:T(4,128)}, u32[]{:S(2)}) copy-start(s32[2,4,108]{2,1,0:T(4,128)} %get-tuple-element.8.local_ref) | copy-start | bytes 10372
  29.2 2.1 %copy-start = (bf16[1,120,2,64,128]{4,3,2,1,0:T(8,128)(2,1)S(1)}, bf16[1,120,2,64,128]{4,3,2,1,0:T(8,128)(2,1)}, u32[]{:S(2)}) copy-start(bf16[1,120,2,64,128]{4,3,2,1,0:T(8,128)(2,1)} %param.4) | copy-start | bytes 11796484
  31.3 1.3 copy-start.1
  173.3 3.9 %collective-permute-start.2 = (f32[4,2,32,64]{3,2,1,0:T(8,128)S(1)}, f32[4,2,32,64]{3,2,1,0:T(8,128)S(1)}, u32[]{:S(2)}, u32[]{:S(2)}) collective-permute-start(f32[4,2,32,64]{3,2,1,0:T(8,128)S(1)} %slice_select_fusion), channel_id=1, source_target_pairs={{0,1},{1,0},{2,3},{3,2},{4,5},{5,4},{6,7},{7,6},{8,9},{9,8},{10,11... | collective-permute-start | bytes 196616 | tf_op jit(solution)/shard_map/ppermute | solution.py:448
  177.2 12.9 %collective-permute-start.3 = (f32[2,2,32,64]{3,2,1,0:T(8,128)S(1)}, f32[2,2,32,64]{3,2,1,0:T(8,128)S(1)}, u32[]{:S(2)}, u32[]{:S(2)}) collective-permute-start(f32[2,2,32,64]{3,2,1,0:T(8,128)S(1)} %slice.62), channel_id=1, source_target_pairs={{8,0},{10,2},{12,4},{14,6},{16,8},{18,10},{20,12},{22,14},{24,16},... | collective-permute-start | bytes 98312 | tf_op jit(solution)/shard_map/ppermute | solution.py:449
  190.1 4.9 %collective-permute-start.4 = (f32[2,32,64]{2,1,0:T(8,128)S(1)}, f32[2,32,64]{2,1,0:T(8,128)S(1)}, u32[]{:S(2)}, u32[]{:S(2)}) collective-permute-start(f32[2,32,64]{2,1,0:T(8,128)S(1)} %get-tuple-element.17), channel_id=1, source_target_pairs={{24,0},{26,2},{28,4},{30,6},{0,8},{2,10},{4,12},{6,14},{8,16},{10,... | collective-permute-start | bytes 49160 | tf_op jit(solution)/shard_map/ppermute | solution.py:450
where the time goes:
time: 196 us
  Pallas kernels  153 us (78%)
  starting transfers between devices  16.2 us (8%)
  waiting for transfers between devices  13 us (7%)
  other arithmetic  6.92 us (4%)
  local copies, waits for them, and re-layouts  5.42 us (3%)
    pallas_call x1, Pallas kernels, meet(): pl.pallas_call(functools.partial(meet_kernel, points, slab, capacity), ou...  141 us
    ppermute x1, starting transfers between devices, on_four_rows(): from_upper = lax.ppermute(total[1:3], 'ka', to_lower)  11.5 us
    pallas_call x1, Pallas kernels, plan(): pl.pallas_call(functools.partial(plan_kernel, slab, capacity), out_shape=...  8.9 us
    ppermute x1, waiting for transfers between devices, on_four_rows(): from_lower = lax.ppermute(total[3], 'ka', to_upper)  4.87 us
    ppermute x1, waiting for transfers between devices, on_four_rows(): lower = lax.ppermute(sent, 'ka', to_upper)  4.14 us
  transfers between devices with their start and end apart: 5, of which 4 were waited for; matrix products, arithmetic and copies ran while one was open for 0% of the time, Pallas kernels for 0%

commit v1 on v0

v1 whole, which is shorter than its diff:
```python
import functools

import jax
import jax.numpy as jnp
from jax import lax
from jax.sharding import PartitionSpec as P
from jax.experimental import pallas as pl
from jax.experimental.pallas import tpu as pltpu

CHUNKS = 10
ROLES = 3


def shifted(block, axis, distance):
    devices = range(lax.axis_size(axis))
    route = [((i - distance) % len(devices), i) for i in devices]
    return lax.ppermute(block, axis, route)


def complex_intersection(bra_real, bra_imag, ket_real, ket_imag, form):
    real_part = jnp.einsum(form, bra_real, ket_real, preferred_element_type=jnp.float32)
    real_part = real_part + jnp.einsum(form, bra_imag, ket_imag, preferred_element_type=jnp.float32)
    imag_part = jnp.einsum(form, bra_real, ket_imag, preferred_element_type=jnp.float32)
    imag_part = imag_part - jnp.einsum(form, bra_imag, ket_real, preferred_element_type=jnp.float32)
    return jnp.stack([real_part, imag_part], axis=-3)


def slot_plan(
    home_slice, target_slice, sent_local, place_local, my_slice, slices, capacity, slab_blocks
):
    targets = jnp.arange(slices, dtype=jnp.int32)
    chosen = (home_slice == my_slice)[:, None, :] & (
        target_slice[:, None, :] == targets[None, :, None]
    )
    chosen = chosen & (targets != my_slice)[None, :, None]
    counted = jnp.cumsum(chosen.astype(jnp.int32), axis=2) - 1
    places = jnp.arange(capacity, dtype=jnp.int32)
    matched = (
        chosen[:, :, None, :] & (counted[:, :, None, :] == places[None, None, :, None])
    ).astype(jnp.int32)
    filled = jnp.sum(matched, axis=3)
    sent_block = jnp.sum(matched * sent_local[:, None, None, :], axis=3)
    where_to = jnp.sum(matched * place_local[:, None, None, :], axis=3) + (1 - filled) * slab_blocks
    pair_count = home_slice.shape[0]
    return (
        sent_block.reshape(pair_count, slices * capacity),
        where_to.reshape(pair_count, slices * capacity),
    )


def on_device(coeffs, neighbour, shift_id, block_map):
    k_local = coeffs.shape[0]
    slab_blocks = coeffs.shape[1]
    band_count = coeffs.shape[3]
    lane_width = coeffs.shape[4]
    vector_count = neighbour.shape[1]
    cycle_size = lax.axis_size("ka")
    slices = lax.axis_size("ga")
    my_cycle = lax.axis_index("ka")
    my_slice = lax.axis_index("ga")
    capacity = 2 * max(1, slab_blocks // 12)
    all_blocks = slab_blocks * slices
    pair_count = k_local * vector_count
    k_total = k_local * cycle_size
    row_points = min(16, k_total // 4)
    row_devices = row_points // k_local
    pad_spec = ((0, 0), (0, 1), (0, 0), (0, 0), (0, 0))
    row_point = shifted(coeffs, "ka", -1)
    row_source = jnp.mod(my_cycle + 1, cycle_size)
    plane_kets = shifted(coeffs, "ka", -row_devices)
    plane_source = jnp.mod(my_cycle + row_devices, cycle_size)
    opposite = shifted(coeffs, "ka", cycle_size // 2)
    targets_flat = neighbour.reshape(-1)
    shifts_flat = shift_id.reshape(-1)
    target_device = targets_flat // k_local
    target_lane = targets_flat - target_device * k_local
    ket_index = jnp.where(
        target_device == my_cycle,
        target_lane,
        jnp.where(
            target_device == row_source,
            k_local,
            jnp.where(
                target_device == plane_source,
                k_local + 1 + target_lane,
                2 * k_local + 1 + target_lane,
            ),
        ),
    )
    bra_index = jnp.arange(pair_count, dtype=jnp.int32) // vector_count
    picks = (
        shifts_flat[:, None] == jnp.arange(block_map.shape[0], dtype=jnp.int32)[None, :]
    ).astype(jnp.int32)
    relabel = jnp.sum(picks[:, :, None] * block_map[None, :, :], axis=1)
    dest_global = jnp.broadcast_to(jnp.arange(all_blocks, dtype=jnp.int32)[None, :], relabel.shape)
    source_slice = relabel // slab_blocks
    dest_slice = dest_global // slab_blocks
    source_local = relabel - source_slice * slab_blocks
    dest_local = dest_global - dest_slice * slab_blocks
    kets = jnp.pad(jnp.concatenate([coeffs, row_point, plane_kets, opposite], axis=0), pad_spec)
    own_source = lax.dynamic_slice_in_dim(relabel, my_slice * slab_blocks, slab_blocks, 1)
    self_place = jnp.where(
        own_source // slab_blocks == my_slice, own_source - my_slice * slab_blocks, slab_blocks
    )
    ket_self = kets[ket_index[:, None], self_place]
    ket_self = ket_self.reshape(k_local, vector_count, slab_blocks, 2, band_count, lane_width)
    local_terms = complex_intersection(
        coeffs[:, :, 0],
        coeffs[:, :, 1],
        ket_self[:, :, :, 0],
        ket_self[:, :, :, 1],
        "ksmw,kbsnw->kbmn",
    )
    sent_block, where_to = slot_plan(
        dest_slice, source_slice, dest_local, source_local, my_slice, slices, capacity, slab_blocks
    )
    payload = coeffs[bra_index[:, None], sent_block]
    owner = jnp.broadcast_to(ket_index[:, None], (pair_count, slices))
    blocks = lax.all_to_all(payload, "ga", split_axis=1, concat_axis=1, tiled=True)
    places_in = lax.all_to_all(where_to, "ga", split_axis=1, concat_axis=1, tiled=True)
    owners = lax.all_to_all(owner, "ga", split_axis=1, concat_axis=1, tiled=True)
    partner = kets[owners[:, 0][:, None], places_in]
    remote = complex_intersection(
        blocks[:, :, 0], blocks[:, :, 1], partner[:, :, 0], partner[:, :, 1], "ismw,isnw->imn"
    )
    summed_part = local_terms + remote.reshape(k_local, vector_count, 2, band_count, band_count)
    total = lax.psum(summed_part, "ga")
    row_count = band_count // slices
    return lax.dynamic_slice_in_dim(total, my_slice * row_count, row_count, 3)


def index_tables(block_map, my_slice, slab, capacity):
    shifts, blocks = block_map.shape
    exact = jnp.bfloat16
    base = (my_slice * slab).astype(jnp.float32)

    def lane_product(left, right, axis):
        return lax.dot_general(
            left.astype(exact), right.astype(exact), (((1,), (axis,)), ((), ())),
            preferred_element_type=jnp.float32,
        )

    def ones(mask):
        return jnp.where(mask, 1.0, 0.0)

    def place_rows(table):
        return lax.broadcasted_iota(jnp.int32, table.shape, 0)

    forward = block_map.astype(jnp.float32)
    counted = lax.broadcasted_iota(jnp.int32, (shifts, blocks), 1).astype(jnp.float32)
    block_rows = lax.broadcasted_iota(jnp.int32, (blocks, blocks), 0)
    inverse = jnp.zeros((shifts, blocks), jnp.float32)
    for r in range(shifts):
        row = lane_product(counted, ones(block_map[r : r + 1, :] == block_rows), 1)
        inverse = jnp.where(place_rows(row) == r, row, inverse)
    before = ones(
        lax.broadcasted_iota(jnp.int32, (slab, slab), 0)
        < lax.broadcasted_iota(jnp.int32, (slab, slab), 1)
    )
    padded = -(-capacity // 8) * 8
    slots = lax.broadcasted_iota(jnp.int32, (padded, slab), 0).astype(jnp.float32)
    indexes, sends = [], []
    for table in (forward, inverse):
        low, high = table[:, :slab], table[:, slab:]
        mine = jnp.where(my_slice == 0, low, high) - base
        other = jnp.where(my_slice == 0, high, low) - base
        inside = (mine >= 0) & (mine < slab)
        rank = jnp.minimum(lane_product(1.0 - ones(inside), before, 0), capacity - 1.0)
        at = jnp.where(inside, mine, slab + rank).astype(jnp.int32)
        indexes.append(jnp.clip(at, 0, slab + capacity - 1))
        wanted = ones((other >= 0) & (other < slab))
        rank = lane_product(wanted, before, 0)
        rank = jnp.where(wanted > 0, rank, -1.0)
        send = jnp.zeros((shifts, padded), jnp.float32)
        for r in range(shifts):
            row = lane_product(other, ones(rank[r : r + 1, :] == slots), 1)
            send = jnp.where(place_rows(row) == r, row, send)
        sends.append(jnp.clip(send.astype(jnp.int32), 0, slab - 1))
    return indexes, sends, padded


def meet_kernel(
    points, slab, capacity, near_ref, shift_ref, map_ref, own_hbm, out_ref,
    own, first, second, third, extra, packs, landed, meta_out, meta_in, tables,
    sums, results, slots, meta, table_at,
    local_sems, meta_sems, send_sems, first_sems, second_sems, third_sems, extra_sems,
    swap_send, swap_recv, result_send, result_recv, go,
):
    levels = points // (points // 4)
    row = points // levels
    me = lax.axis_index("ka")
    my_slice = lax.axis_index("ga")
    partner = 1 - my_slice
    z, column = me // row, me % row
    low = (column == 0) | (column == row - 1)
    role = jnp.where(low, z, levels - 1 - z)
    is_outer, is_hub, is_inner, is_far = role == 0, role == 1, role == 2, role == 3

    def member(r):
        return jnp.where(low, r, levels - 1 - r) * row + column

    outer, hub, inner, far = member(0), member(1), member(2), member(3)
    twin = me + 1 - 2 * (column % 2)
    lower_half = z < 2
    bands, lanes = own.shape[2], own.shape[3]
    size = slab // CHUNKS
    shifts = map_ref.shape[0]

    barrier = pltpu.get_barrier_semaphore()
    mesh = pl.DeviceIdType.MESH

    def greet(r, carry):
        peer = (me + r) % points
        for g in range(2):
            pl.semaphore_signal(barrier, inc=1, device_id={"ka": peer, "ga": g}, device_id_type=mesh)
        return carry

    lax.fori_loop(1, points, greet, 0)
    pl.semaphore_signal(barrier, inc=1, device_id={"ga": partner}, device_id_type=mesh)
    pl.semaphore_wait(barrier, 2 * points - 1)

    def remote(source, target, send, recv, peer):
        return pltpu.make_async_remote_copy(
            src_ref=source, dst_ref=target, send_sem=send, recv_sem=recv,
            device_id=peer, device_id_type=mesh,
        )

    def chunk(c):
        return pl.ds(c * size, size)

    def own_part(c, target, n, sems, peer):
        return remote(own_hbm.at[chunk(c)], target.at[chunk(c)], send_sems.at[n], sems.at[c], {"ka": peer})

    def send_own(target, n, sems, peer, start=0, stop=CHUNKS):
        for c in range(start, stop):
            own_part(c, target, n, sems, peer).start()

    def sent_own(n, chunks):
        part = own_hbm.at[pl.ds(0, chunks * size)]
        return remote(part, own.at[pl.ds(0, chunks * size)], send_sems.at[n], first_sems.at[0], {"ka": twin})

    keep = pltpu.make_async_copy(own_hbm, own.at[pl.ds(0, slab)], local_sems.at[0])

    @pl.when(is_outer)
    def _():
        send_own(first, 0, first_sems, hub, 0, CHUNKS - 1)
        send_own(first, 1, first_sems, hub, CHUNKS - 1, CHUNKS)

    @pl.when(is_inner)
    def _():
        send_own(second, 0, second_sems, hub, 0, CHUNKS - 1)
        send_own(second, 1, second_sems, hub, CHUNKS - 1, CHUNKS)

    corner_low = me == row
    corner_high = me == 2 * row - 1
    gated_extra = me == row + 2
    extra_down = (me == row) | (me == 2)
    extra_up = (me == 2 * row + 1) | (me == 2 * row + 3) | (me == 3 * row + 1)
    extra_source = extra_down | extra_up | corner_high | gated_extra
    extra_site = (
        (me == row - 1) | (me == 1) | (me == row + 1)
        | (me == 2 * row + 2) | (me == 3 * row) | (me == 3 * row + 2)
    )
    extra_peer = jnp.where(corner_high, row, jnp.where(extra_up, me + 1, me - 1))

    @pl.when(extra_down | extra_up | corner_high)
    def _():
        send_own(extra, 3, extra_sems, extra_peer)

    @pl.when(is_outer | is_hub)
    def _():
        send_own(first, 2, first_sems, twin)

    keep.start()

    def role_shift(step):
        target = (me + step) % points
        total = jnp.int32(0)
        for b in range(ROLES):
            total = total + jnp.where(near_ref[0, b] == target, shift_ref[0, b], 0)
        return total

    lane = lax.broadcasted_iota(jnp.int32, meta_out.shape, 1)
    facts = jnp.where(
        lane == 0, role_shift(1), jnp.where(lane == 1, role_shift(row), role_shift(points // 2))
    )
    meta_out[...] = facts
    meta_in[me] = facts

    indexes, sends, padded = index_tables(map_ref[...], my_slice, slab, capacity)
    tables[...] = jnp.zeros_like(tables)
    for d in range(2):
        tables[pl.ds(d * shifts, shifts), pl.ds(0, slab)] = indexes[d]
        tables[pl.ds((2 + d) * shifts, shifts), pl.ds(0, padded)] = sends[d]

    def tell(r, carry):
        remote(meta_out, meta_in.at[me], meta_sems.at[0], meta_sems.at[1], {"ka": (me + r) % points}).start()
        return carry

    lax.fori_loop(1, points, tell, 0)
    told = meta_in.at[pl.ds(0, points - 1)]
    all_told = remote(told, told, meta_sems.at[0], meta_sems.at[1], {"ka": twin})
    tables_in = pltpu.make_async_copy(tables, table_at, local_sems.at[1])
    tables_in.start()
    all_told.wait_recv()
    meta_copy = pltpu.make_async_copy(meta_in, meta, local_sems.at[2])
    meta_copy.start()
    all_told.wait_send()
    meta_copy.wait()
    tables_in.wait()
    keep.wait()

    def shift_of(point, kind):
        return meta[point, 0, kind]

    NEXT, ROW, HALF = 0, 1, 2

    def swap(n):
        part = pl.ds(n * capacity, capacity)
        return remote(packs.at[part], landed.at[part], swap_send.at[n], swap_recv.at[n], {"ga": partner})

    def take(n, target, place):
        swap(n).wait_recv()

        def move(r, carry):
            target[slab + place * capacity + r] = landed[n * capacity + r]
            return carry

        lax.fori_loop(0, capacity, move, 0, unroll=4)

    def pack(n, source, inverse, shift):
        line = (2 + inverse) * shifts + shift

        def gather(r, carry):
            packs[n * capacity + r] = source[table_at[line, r]]
            return carry

        lax.fori_loop(0, capacity, gather, 0, unroll=4)

    def offer(n, source, inverse, shift):
        pack(n, source, inverse, shift)
        swap(n).start()

    def pick(ref, at):
        return ref[at].reshape(2 * bands, lanes)

    def accumulate(e, c, still, moving, place, inverse, shift):
        line = inverse * shifts + shift

        def at(n):
            value = table_at[line, n]
            return value + jnp.where(value >= slab, place * capacity, 0)

        total = sums[e]
        for u in range(0, size, 2):
            n = c * size + u
            total = total + lax.dot_general(
                jnp.concatenate([pick(still, n), pick(still, n + 1)], axis=1),
                jnp.concatenate([pick(moving, at(n)), pick(moving, at(n + 1))], axis=1),
                (((1,), (1,)), ((), ())),
                preferred_element_type=jnp.float32,
            )
        sums[e] = total

    def whole(e, still, moving, place, inverse, shift):
        def step(c, carry):
            accumulate(e, c, still, moving, place, inverse, shift)
            return carry

        lax.fori_loop(0, CHUNKS, step, 0)

    def result_copies(e, kind, bra):
        pairs = []
        half = bands // 2
        for g in range(2):
            source = results.at[e, pl.ds(g * half, half)]
            target = slots.at[kind, my_slice]
            arrived = result_recv.at[kind * 2 + my_slice]
            at_home = (bra == me) & (my_slice == g)
            near = pltpu.make_async_copy(source, target, arrived)
            away = remote(source, target, result_send.at[e * 2 + g], arrived, {"ka": bra, "ga": g})
            pairs.append((at_home, near, away))
        return pairs

    def deliver(e, kind, bra, inverse):
        total = sums[e]
        total = jnp.where(inverse == 1, total.T, total)
        upper, under = total[:bands], pltpu.roll(total[bands:], bands, 1)
        left = lax.broadcasted_iota(jnp.int32, upper.shape, 1) < bands
        results[e] = upper + jnp.where(left, under, -under)
        for at_home, near, away in result_copies(e, kind, bra):
            pl.when(at_home)(near.start)
            pl.when(~at_home)(away.start)

    def delivered(e, kind, bra):
        for at_home, _, away in result_copies(e, kind, bra):
            pl.when(~at_home)(away.wait_send)

    def arrived(buffer, sems, c):
        part = buffer.at[chunk(c)]
        remote(part, part, send_sems.at[0], sems.at[c], {"ka": twin}).wait_recv()

    sums[...] = jnp.zeros_like(sums)
    flip = jnp.where(low, 0, 1)
    extra_inverse = jnp.where(lower_half, 1, 0)
    extra_bra = jnp.where(lower_half, me, me - 1)
    EXTRA = 6
    OWN_EXTRA = 4
    OUTER_SLOT, INNER_SLOT, CORNER_SLOT = 5, 6, 7

    hub_edges = (
        (first, own, 0, flip, jnp.where(low, outer, hub), ROW),
        (second, own, 1, 1 - flip, jnp.where(low, hub, inner), ROW),
        (third, own, 2, 1, hub, HALF),
        (third, own, 3, 0, far, HALF),
        (third, first, 0, flip, jnp.where(low, far, outer), ROW),
        (third, second, 0, 1 - flip, jnp.where(low, inner, far), ROW),
    )

    @pl.when(extra_site)
    def _():
        offer(OWN_EXTRA, own, extra_inverse, shift_of(extra_bra, NEXT))

    def extra_edge():
        take(OWN_EXTRA, own, OWN_EXTRA)
        shift = shift_of(extra_bra, NEXT)

        def step(c, carry):
            arrived(extra, extra_sems, c)
            accumulate(EXTRA, c, extra, own, OWN_EXTRA, extra_inverse, shift)
            return carry

        lax.fori_loop(0, CHUNKS, step, 0)
        deliver(EXTRA, NEXT, extra_bra, extra_inverse)

    def corner_copy(c):
        return remote(first.at[chunk(c)], extra.at[chunk(c)], send_sems.at[5], extra_sems.at[c], {"ka": 2 * row - 1})

    @pl.when(is_hub)
    def _():
        for e in range(4):
            _, _, _, inverse, bra, kind = hub_edges[e]
            offer(e, own, inverse, shift_of(bra, kind))

        def relay(c, carry):
            arrived(second, second_sems, c)
            remote(second.at[chunk(c)], first.at[chunk(c)], send_sems.at[4], first_sems.at[c], {"ka": outer}).start()
            arrived(first, first_sems, c)
            pl.when(corner_low)(corner_copy(c).start)
            return carry

        lax.fori_loop(0, CHUNKS, relay, 0)

        @pl.when(corner_high)
        def _():
            sent_own(3, CHUNKS).wait_send()
            pl.semaphore_signal(go, inc=1, device_id={"ka": twin}, device_id_type=mesh)

        for n, e in ((OUTER_SLOT, 4), (INNER_SLOT, 5)):
            _, source, _, inverse, bra, kind = hub_edges[e]
            offer(n, source, inverse, shift_of(bra, kind))

        @pl.when(corner_low)
        def _():
            offer(CORNER_SLOT, second, 0, shift_of(2 * row - 1, NEXT))

        for e in range(2):
            still, moving, place, inverse, bra, kind = hub_edges[e]
            take(e, own, e)
            whole(e, still, moving, place, inverse, shift_of(bra, kind))
            deliver(e, kind, bra, inverse)

        @pl.when(extra_site)
        def _():
            extra_edge()

        @pl.when(corner_high)
        def _():
            def gain(c, carry):
                arrived(extra, extra_sems, c)
                return carry

            lax.fori_loop(0, CHUNKS, gain, 0)
            offer(CORNER_SLOT, extra, 0, shift_of(4 * row - 1, NEXT))

        for e in (2, 3):
            take(e, own, e)
        take(OUTER_SLOT, first, 0)
        take(INNER_SLOT, second, 0)

        @pl.when(corner_low)
        def _():
            take(CORNER_SLOT, second, 1)

            def step(c, carry):
                arrived(extra, extra_sems, c)
                accumulate(EXTRA, c, extra, second, 1, 0, shift_of(2 * row - 1, NEXT))
                return carry

            lax.fori_loop(0, CHUNKS, step, 0)
            deliver(EXTRA, NEXT, 2 * row - 1, 0)

        @pl.when(corner_high)
        def _():
            take(CORNER_SLOT, extra, 0)

        def late(c, carry):
            arrived(third, third_sems, c)
            for e in range(2, 6):
                still, moving, place, inverse, bra, kind = hub_edges[e]
                accumulate(e, c, still, moving, place, inverse, shift_of(bra, kind))

            @pl.when(corner_high)
            def _():
                accumulate(EXTRA, c, third, extra, 0, 0, shift_of(4 * row - 1, NEXT))

            return carry

        lax.fori_loop(0, CHUNKS, late, 0)
        for e in range(2, 6):
            _, _, _, inverse, bra, kind = hub_edges[e]
            deliver(e, kind, bra, inverse)

        @pl.when(corner_high)
        def _():
            deliver(EXTRA, NEXT, 4 * row - 1, 0)

        for e in range(6):
            _, _, _, _, bra, kind = hub_edges[e]
            delivered(e, kind, bra)

        @pl.when(corner_low)
        def _():
            delivered(EXTRA, NEXT, 2 * row - 1)
            swap(CORNER_SLOT).wait_send()
            sent_own(5, CHUNKS).wait_send()

        @pl.when(corner_high)
        def _():
            delivered(EXTRA, NEXT, 4 * row - 1)
            swap(CORNER_SLOT).wait_send()

        for e in range(4):
            swap(e).wait_send()
        swap(OUTER_SLOT).wait_send()
        swap(INNER_SLOT).wait_send()
        sent_own(4, CHUNKS).wait_send()

    @pl.when(is_outer)
    def _():
        for e, inverse, bra in ((0, 1, outer), (1, 0, inner)):
            offer(e, own, inverse, shift_of(bra, HALF))
        sent_own(0, CHUNKS - 1).wait_send()
        pl.semaphore_signal(go, inc=1, device_id={"ka": twin}, device_id_type=mesh)
        for e in range(2):
            take(e, own, e)

        def step(c, carry):
            arrived(first, first_sems, c)
            for e, inverse, bra in ((0, 1, outer), (1, 0, inner)):
                accumulate(e, c, first, own, e, inverse, shift_of(bra, HALF))
            return carry

        lax.fori_loop(0, CHUNKS, step, 0)
        for e, inverse, bra in ((0, 1, outer), (1, 0, inner)):
            deliver(e, HALF, bra, inverse)
        pl.when(extra_site)(extra_edge)
        for e, inverse, bra in ((0, 1, outer), (1, 0, inner)):
            delivered(e, HALF, bra)
            swap(e).wait_send()

    twin_inverse = jnp.where(column % 2 == 1, 0, 1)
    twin_bra = me - column % 2

    @pl.when(is_inner | is_far)
    def _():
        shift = shift_of(twin_bra, NEXT)
        offer(0, own, twin_inverse, shift)
        take(0, own, 0)

        def step(c, carry):
            arrived(first, first_sems, c)
            accumulate(0, c, first, own, 0, twin_inverse, shift)
            return carry

        lax.fori_loop(0, CHUNKS, step, 0)
        deliver(0, NEXT, twin_bra, twin_inverse)

        @pl.when(is_far | gated_extra)
        def _():
            pl.semaphore_wait(go, 1)

        @pl.when(is_far)
        def _():
            send_own(third, 0, third_sems, hub, 0, CHUNKS - 1)
            send_own(third, 1, third_sems, hub, CHUNKS - 1, CHUNKS)

        @pl.when(gated_extra)
        def _():
            send_own(extra, 3, extra_sems, extra_peer)

        pl.when(extra_site)(extra_edge)
        delivered(0, NEXT, twin_bra)
        swap(0).wait_send()
        sent_own(0, CHUNKS - 1).wait_send()

    @pl.when(extra_site)
    def _():
        delivered(EXTRA, NEXT, extra_bra)
        swap(OWN_EXTRA).wait_send()

    @pl.when(~is_hub)
    def _():
        sent_own(1, 1).wait_send()

    @pl.when(is_outer | is_hub)
    def _():
        sent_own(2, CHUNKS).wait_send()

    @pl.when(extra_source)
    def _():
        @pl.when(~corner_high)
        def _():
            sent_own(3, CHUNKS).wait_send()

    for kind in range(ROLES):
        for g in range(2):
            slot = slots.at[kind, g]
            pltpu.make_async_copy(slot, slot, result_recv.at[kind * 2 + g]).wait()
        both = slots[kind, 0] + slots[kind, 1]
        out_ref[kind, 0] = both[:, :bands]
        out_ref[kind, 1] = both[:, bands:]


def meet(neighbour, shift_id, block_map, own, points, capacity):
    slab, bands, lanes = own.shape[0], own.shape[2], own.shape[3]
    block = own.shape[1:]
    shifts = block_map.shape[0]
    half = bands // 2
    dma = pltpu.SemaphoreType.DMA

    def blocks(count):
        return pltpu.VMEM((count,) + block, own.dtype)

    return pl.pallas_call(
        functools.partial(meet_kernel, points, slab, capacity),
        out_shape=jax.ShapeDtypeStruct((ROLES, 2, half, bands), jnp.float32),
        in_specs=[
            pl.BlockSpec(memory_space=pltpu.SMEM),
            pl.BlockSpec(memory_space=pltpu.SMEM),
            pl.BlockSpec(memory_space=pltpu.VMEM),
            pl.BlockSpec(memory_space=pl.ANY),
        ],
        out_specs=pl.BlockSpec(memory_space=pltpu.VMEM),
        scratch_shapes=[
            blocks(slab + 5 * capacity),
            blocks(slab + capacity),
            blocks(slab + 2 * capacity),
            blocks(slab),
            blocks(slab + capacity),
            blocks(8 * capacity),
            blocks(8 * capacity),
            pltpu.VMEM((1, lanes), jnp.int32),
            pltpu.VMEM((points, 1, lanes), jnp.int32),
            pltpu.VMEM((4 * shifts, lanes), jnp.int32),
            pltpu.VMEM((7, 2 * bands, 2 * bands), jnp.float32),
            pltpu.VMEM((7, bands, 2 * bands), jnp.float32),
            pltpu.VMEM((ROLES, 2, half, 2 * bands), jnp.float32),
            pltpu.SMEM((points, 1, lanes), jnp.int32),
            pltpu.SMEM((4 * shifts, lanes), jnp.int32),
            dma((3,)), dma((2,)), dma((6,)),
            dma((CHUNKS,)), dma((CHUNKS,)), dma((CHUNKS,)), dma((CHUNKS,)),
            dma((8,)), dma((8,)), dma((14,)), dma((2 * ROLES,)),
            pltpu.SemaphoreType.REGULAR,
        ],
        compiler_params=pltpu.CompilerParams(
            collective_id=0, has_side_effects=True, vmem_limit_bytes=60 * 2**20
        ),
        name="meet",
    )(neighbour, shift_id, block_map, own)


def on_four_levels(coeffs, neighbour, shift_id, block_map):
    own = coeffs[0]
    points = lax.axis_size("ka")
    row = points // 4
    me = lax.axis_index("ka")
    capacity = 2 * max(1, own.shape[0] // 12)
    sums = meet(neighbour, shift_id, block_map, own, points, capacity)
    target = neighbour[0][:, None, None, None]
    out = jnp.where(
        target == jnp.mod(me + 1, points),
        sums[0],
        jnp.where(target == jnp.mod(me + row, points), sums[1], sums[2]),
    )
    return out[None]


def solution(mesh):
    in_specs = (P("ka", "ga", None, None, None), P("ka", None), P("ka", None), P())
    out_specs = P("ka", None, None, "ga", None)
    levels = mesh.shape["ka"] // 4
    square = mesh.shape["ga"] == 2 and mesh.shape["ka"] == 4 * levels and levels == 4

    def run(coeffs, neighbour, shift_id, block_map):
        one_each = coeffs.shape[0] == mesh.shape["ka"] and neighbour.shape[1] == ROLES
        per_slice = coeffs.shape[1] // mesh.shape["ga"]
        lanes = coeffs.shape[4]
        fits = per_slice % (2 * CHUNKS) == 0 and per_slice <= lanes and 2 * coeffs.shape[3] == lanes
        body = on_four_levels if square and one_each and fits else on_device
        return jax.shard_map(
            body, mesh=mesh, in_specs=in_specs, out_specs=out_specs, check_vma=False
        )(coeffs, neighbour, shift_id, block_map)

    return run
```

time: 196 us -> 139 us (0.71)
  the two profiles are of different devices: /device:TPU:5 before, /device:TPU:16 now
where the time goes in v1:
time: 139 us; the launch traced here: 138 us
  Pallas kernels  137 us (99%)
    pallas_call x1, Pallas kernels, meet(): pl.pallas_call(functools.partial(meet_kernel, points, slab, capacity), ou...  137 us

profile of v1, /device:TPU:16, one launch (start us, length us, event | category | flops | bytes accessed | tf_op | source)
XLA Modules:
  0.0 138.3 jit_solution(17090697505143149188)
XLA Ops:
  0.0 0.0 copy-start
  0.0 136.7 %meet.1 = f32[3,2,32,64]{3,2,1,0:T(8,128)} custom-call(s32[1,3]{1,0:T(1,128)} %near_ref.1, s32[1,3]{1,0:T(1,128)} %shift_ref.1, s32[8,240]{1,0:T(8,128)} %map_ref.1, bf16[120,2,64,128]{3,2,1,0:T(8,128)(2,1)} %bitcast.11), custom_call_target="tpu_custom_call" | custom-call | tf_op jit(solution)/shard_map/meet/pallas_call | solution.py:645
  136.8 0.8 slice_bitcast_fusion.2
  137.6 0.0 copy-done
  137.6 0.7 select_select_fusion
  (1 shorter events, 0.0 us)
Async XLA Ops:
  0.0 137.6 %copy-start = (s32[1,3]{1,0:T(1,128)S(1)}, s32[1,3]{1,0:T(1,128)}, u32[]{:S(2)}) copy-start(s32[1,3]{1,0:T(1,128)} %near_ref.1) | copy-start | bytes 40

commit v2 on v1

--- a/solution.py
+++ b/solution.py
@@ -215,64 +215,6 @@
             pl.semaphore_signal(barrier, inc=1, device_id={"ka": peer, "ga": g}, device_id_type=mesh)
         return carry
 
-    lax.fori_loop(1, points, greet, 0)
-    pl.semaphore_signal(barrier, inc=1, device_id={"ga": partner}, device_id_type=mesh)
-    pl.semaphore_wait(barrier, 2 * points - 1)
-
-    def remote(source, target, send, recv, peer):
-        return pltpu.make_async_remote_copy(
-            src_ref=source, dst_ref=target, send_sem=send, recv_sem=recv,
-            device_id=peer, device_id_type=mesh,
-        )
-
-    def chunk(c):
-        return pl.ds(c * size, size)
-
-    def own_part(c, target, n, sems, peer):
-        return remote(own_hbm.at[chunk(c)], target.at[chunk(c)], send_sems.at[n], sems.at[c], {"ka": peer})
-
-    def send_own(target, n, sems, peer, start=0, stop=CHUNKS):
-        for c in range(start, stop):
-            own_part(c, target, n, sems, peer).start()
-
-    def sent_own(n, chunks):
-        part = own_hbm.at[pl.ds(0, chunks * size)]
-        return remote(part, own.at[pl.ds(0, chunks * size)], send_sems.at[n], first_sems.at[0], {"ka": twin})
-
-    keep = pltpu.make_async_copy(own_hbm, own.at[pl.ds(0, slab)], local_sems.at[0])
-
-    @pl.when(is_outer)
-    def _():
-        send_own(first, 0, first_sems, hub, 0, CHUNKS - 1)
-        send_own(first, 1, first_sems, hub, CHUNKS - 1, CHUNKS)
-
-    @pl.when(is_inner)
-    def _():
-        send_own(second, 0, second_sems, hub, 0, CHUNKS - 1)
-        send_own(second, 1, second_sems, hub, CHUNKS - 1, CHUNKS)
-
-    corner_low = me == row
-    corner_high = me == 2 * row - 1
-    gated_extra = me == row + 2
-    extra_down = (me == row) | (me == 2)
-    extra_up = (me == 2 * row + 1) | (me == 2 * row + 3) | (me == 3 * row + 1)
-    extra_source = extra_down | extra_up | corner_high | gated_extra
-    extra_site = (
-        (me == row - 1) | (me == 1) | (me == row + 1)
-        | (me == 2 * row + 2) | (me == 3 * row) | (me == 3 * row + 2)
-    )
-    extra_peer = jnp.where(corner_high, row, jnp.where(extra_up, me + 1, me - 1))
-
-    @pl.when(extra_down | extra_up | corner_high)
-    def _():
-        send_own(extra, 3, extra_sems, extra_peer)
-
-    @pl.when(is_outer | is_hub)
-    def _():
-        send_own(first, 2, first_sems, twin)
-
-    keep.start()
-
     def role_shift(step):
         target = (me + step) % points
         total = jnp.int32(0)
@@ -280,12 +222,71 @@
             total = total + jnp.where(near_ref[0, b] == target, shift_ref[0, b], 0)
         return total
 
+    keep = pltpu.make_async_copy(own_hbm, own.at[pl.ds(0, slab)], local_sems.at[0])
+    keep.start()
     lane = lax.broadcasted_iota(jnp.int32, meta_out.shape, 1)
     facts = jnp.where(
         lane == 0, role_shift(1), jnp.where(lane == 1, role_shift(row), role_shift(points // 2))
     )
     meta_out[...] = facts
     meta_in[me] = facts
+
+    lax.fori_loop(1, points, greet, 0)
+    pl.semaphore_signal(barrier, inc=1, device_id={"ga": partner}, device_id_type=mesh)
+    pl.semaphore_wait(barrier, 2 * points - 1)
+
+    def remote(source, target, send, recv, peer):
+        return pltpu.make_async_remote_copy(
+            src_ref=source, dst_ref=target, send_sem=send, recv_sem=recv,
+            device_id=peer, device_id_type=mesh,
+        )
+
+    def chunk(c):
+        return pl.ds(c * size, size)
+
+    def own_part(c, target, n, sems, peer):
+        return remote(own_hbm.at[chunk(c)], target.at[chunk(c)], send_sems.at[n], sems.at[c], {"ka": peer})
+
+    def send_own(target, n, sems, peer):
+        for c in range(CHUNKS):
+            own_part(c, target, n, sems, peer).start()
+
+    def sent_own(n):
+        return remote(own_hbm, own.at[pl.ds(0, slab)], send_sems.at[n], first_sems.at[0], {"ka": twin})
+
+    def tell(r, carry):
+        remote(meta_out, meta_in.at[me], meta_sems.at[0], meta_sems.at[1], {"ka": (me + r) % points}).start()
+        return carry
+
+    lax.fori_loop(1, points, tell, 0)
+
+    @pl.when(is_outer)
+    def _():
+        send_own(first, 0, first_sems, hub)
+
+    @pl.when(is_inner)
+    def _():
+        send_own(second, 0, second_sems, hub)
+
+    corner_low = me == row
+    corner_high = me == 2 * row - 1
+    gated_extra = me == row + 2
+    extra_down = me == 2
+    extra_up = (me == 2 * row + 1) | (me == 2 * row + 3) | (me == 3 * row + 1)
+    extra_source = extra_down | extra_up | corner_low | gated_extra
+    extra_site = (
+        (me == row - 1) | (me == 1) | (me == row + 1)
+        | (me == 2 * row + 2) | (me == 3 * row) | (me == 3 * row + 2)
+    )
+    extra_peer = jnp.where(corner_high, row, jnp.where(extra_up, me + 1, me - 1))
+
+    @pl.when(extra_down | extra_up | corner_high)
+    def _():
+        send_own(extra, 3, extra_sems, extra_peer)
+
+    @pl.when(is_outer | is_hub)
+    def _():
+        send_own(first, 2, first_sems, twin)
 
     indexes, sends, padded = index_tables(map_ref[...], my_slice, slab, capacity)
     tables[...] = jnp.zeros_like(tables)
@@ -293,11 +294,6 @@
         tables[pl.ds(d * shifts, shifts), pl.ds(0, slab)] = indexes[d]
         tables[pl.ds((2 + d) * shifts, shifts), pl.ds(0, padded)] = sends[d]
 
-    def tell(r, carry):
-        remote(meta_out, meta_in.at[me], meta_sems.at[0], meta_sems.at[1], {"ka": (me + r) % points}).start()
-        return carry
-
-    lax.fori_loop(1, points, tell, 0)
     told = meta_in.at[pl.ds(0, points - 1)]
     all_told = remote(told, told, meta_sems.at[0], meta_sems.at[1], {"ka": twin})
     tables_in = pltpu.make_async_copy(tables, table_at, local_sems.at[1])
@@ -451,9 +447,13 @@
 
         lax.fori_loop(0, CHUNKS, relay, 0)
 
+        @pl.when(corner_low)
+        def _():
+            send_own(extra, 3, extra_sems, extra_peer)
+
         @pl.when(corner_high)
         def _():
-            sent_own(3, CHUNKS).wait_send()
+            sent_own(3).wait_send()
             pl.semaphore_signal(go, inc=1, device_id={"ka": twin}, device_id_type=mesh)
 
         for n, e in ((OUTER_SLOT, 4), (INNER_SLOT, 5)):
@@ -533,7 +533,7 @@
         def _():
             delivered(EXTRA, NEXT, 2 * row - 1)
             swap(CORNER_SLOT).wait_send()
-            sent_own(5, CHUNKS).wait_send()
+            sent_own(5).wait_send()
 
         @pl.when(corner_high)
         def _():
@@ -544,13 +544,13 @@
             swap(e).wait_send()
         swap(OUTER_SLOT).wait_send()
         swap(INNER_SLOT).wait_send()
-        sent_own(4, CHUNKS).wait_send()
+        sent_own(4).wait_send()
 
     @pl.when(is_outer)
     def _():
         for e, inverse, bra in ((0, 1, outer), (1, 0, inner)):
             offer(e, own, inverse, shift_of(bra, HALF))
-        sent_own(0, CHUNKS - 1).wait_send()
+        sent_own(0).wait_send()
         pl.semaphore_signal(go, inc=1, device_id={"ka": twin}, device_id_type=mesh)
         for e in range(2):
             take(e, own, e)
@@ -586,14 +586,19 @@
         lax.fori_loop(0, CHUNKS, step, 0)
         deliver(0, NEXT, twin_bra, twin_inverse)
 
-        @pl.when(is_far | gated_extra)
+        @pl.when(is_inner)
+        def _():
+            sent_own(0).wait_send()
+            pl.semaphore_signal(go, inc=1, device_id={"ka": far}, device_id_type=mesh)
+
+        @pl.when(gated_extra)
         def _():
             pl.semaphore_wait(go, 1)
 
         @pl.when(is_far)
         def _():
-            send_own(third, 0, third_sems, hub, 0, CHUNKS - 1)
-            send_own(third, 1, third_sems, hub, CHUNKS - 1, CHUNKS)
+            pl.semaphore_wait(go, 2)
+            send_own(third, 0, third_sems, hub)
 
         @pl.when(gated_extra)
         def _():
@@ -602,26 +607,20 @@
         pl.when(extra_site)(extra_edge)
         delivered(0, NEXT, twin_bra)
         swap(0).wait_send()
-        sent_own(0, CHUNKS - 1).wait_send()
+        pl.when(is_far)(sent_own(0).wait_send)
 
     @pl.when(extra_site)
     def _():
         delivered(EXTRA, NEXT, extra_bra)
         swap(OWN_EXTRA).wait_send()
 
-    @pl.when(~is_hub)
-    def _():
-        sent_own(1, 1).wait_send()
-
     @pl.when(is_outer | is_hub)
     def _():
-        sent_own(2, CHUNKS).wait_send()
+        sent_own(2).wait_send()
 
     @pl.when(extra_source)
     def _():
-        @pl.when(~corner_high)
-        def _():
-            sent_own(3, CHUNKS).wait_send()
+        sent_own(3).wait_send()
 
     for kind in range(ROLES):
         for g in range(2):

time: 139 us -> 106 us (0.76)
  the two profiles are of different devices: /device:TPU:16 before, /device:TPU:5 now
where the time goes in v2:
time: 106 us; the launch traced here: 105 us
  Pallas kernels  104 us (98%)
    pallas_call x1, Pallas kernels, meet(): pl.pallas_call(functools.partial(meet_kernel, points, slab, capacity), ou...  104 us

profile of v2, /device:TPU:5, one launch (start us, length us, event | category | flops | bytes accessed | tf_op | source)
XLA Modules:
  0.0 105.4 jit_solution(7043873736635333715)
XLA Ops:
  0.0 0.0 copy-start
  0.0 103.9 %meet.1 = f32[3,2,32,64]{3,2,1,0:T(8,128)} custom-call(s32[1,3]{1,0:T(1,128)} %near_ref.1, s32[1,3]{1,0:T(1,128)} %shift_ref.1, s32[8,240]{1,0:T(8,128)} %map_ref.1, bf16[120,2,64,128]{3,2,1,0:T(8,128)(2,1)} %bitcast.11), custom_call_target="tpu_custom_call" | custom-call | tf_op jit(solution)/shard_map/meet/pallas_call | solution.py:644
  103.9 0.8 slice_bitcast_fusion.2
  104.7 0.0 copy-done
  104.7 0.7 select_select_fusion
  (1 shorter events, 0.0 us)
Async XLA Ops:
  0.0 104.7 %copy-start = (s32[1,3]{1,0:T(1,128)S(1)}, s32[1,3]{1,0:T(1,128)}, u32[]{:S(2)}) copy-start(s32[1,3]{1,0:T(1,128)} %near_ref.1) | copy-start | bytes 40

commit v3 on v2

--- a/solution.py
+++ b/solution.py
@@ -7,7 +7,9 @@
 from jax.experimental import pallas as pl
 from jax.experimental.pallas import tpu as pltpu
 
-CHUNKS = 10
+CHUNKS = 20
+EARLY = 3
+LUMP = 4
 ROLES = 3
 
 
@@ -180,8 +182,8 @@
 
 
 def meet_kernel(
-    points, slab, capacity, near_ref, shift_ref, map_ref, own_hbm, out_ref,
-    own, first, second, third, extra, packs, landed, meta_out, meta_in, tables,
+    points, slab, capacity, near_hbm, shift_hbm, map_hbm, own_hbm, out_ref,
+    near_ref, shift_ref, map_ref, own, first, second, third, extra, packs, landed, meta_out, meta_in, tables,
     sums, results, slots, meta, table_at,
     local_sems, meta_sems, send_sems, first_sems, second_sems, third_sems, extra_sems,
     swap_send, swap_recv, result_send, result_recv, go,
@@ -200,11 +202,12 @@
         return jnp.where(low, r, levels - 1 - r) * row + column
 
     outer, hub, inner, far = member(0), member(1), member(2), member(3)
+    below, above = hub - row, hub + row
     twin = me + 1 - 2 * (column % 2)
     lower_half = z < 2
     bands, lanes = own.shape[2], own.shape[3]
     size = slab // CHUNKS
-    shifts = map_ref.shape[0]
+    shifts = map_hbm.shape[0]
 
     barrier = pltpu.get_barrier_semaphore()
     mesh = pl.DeviceIdType.MESH
@@ -214,6 +217,17 @@
         for g in range(2):
             pl.semaphore_signal(barrier, inc=1, device_id={"ka": peer, "ga": g}, device_id_type=mesh)
         return carry
+
+    lax.fori_loop(1, points, greet, 0)
+    pl.semaphore_signal(barrier, inc=1, device_id={"ga": partner}, device_id_type=mesh)
+    near_in = pltpu.make_async_copy(near_hbm, near_ref, local_sems.at[3])
+    shift_in = pltpu.make_async_copy(shift_hbm, shift_ref, local_sems.at[4])
+    map_in = pltpu.make_async_copy(map_hbm, map_ref, local_sems.at[5])
+    keep = pltpu.make_async_copy(own_hbm, own.at[pl.ds(0, slab)], local_sems.at[0])
+    for copy in (near_in, shift_in, map_in, keep):
+        copy.start()
+    near_in.wait()
+    shift_in.wait()
 
     def role_shift(step):
         target = (me + step) % points
@@ -222,17 +236,12 @@
             total = total + jnp.where(near_ref[0, b] == target, shift_ref[0, b], 0)
         return total
 
-    keep = pltpu.make_async_copy(own_hbm, own.at[pl.ds(0, slab)], local_sems.at[0])
-    keep.start()
     lane = lax.broadcasted_iota(jnp.int32, meta_out.shape, 1)
     facts = jnp.where(
         lane == 0, role_shift(1), jnp.where(lane == 1, role_shift(row), role_shift(points // 2))
     )
     meta_out[...] = facts
     meta_in[me] = facts
-
-    lax.fori_loop(1, points, greet, 0)
-    pl.semaphore_signal(barrier, inc=1, device_id={"ga": partner}, device_id_type=mesh)
     pl.semaphore_wait(barrier, 2 * points - 1)
 
     def remote(source, target, send, recv, peer):
@@ -247,12 +256,13 @@
     def own_part(c, target, n, sems, peer):
         return remote(own_hbm.at[chunk(c)], target.at[chunk(c)], send_sems.at[n], sems.at[c], {"ka": peer})
 
-    def send_own(target, n, sems, peer):
-        for c in range(CHUNKS):
+    def send_own(target, n, sems, peer, start=0, stop=CHUNKS):
+        for c in range(start, stop):
             own_part(c, target, n, sems, peer).start()
 
-    def sent_own(n):
-        return remote(own_hbm, own.at[pl.ds(0, slab)], send_sems.at[n], first_sems.at[0], {"ka": twin})
+    def sent_own(n, chunks=CHUNKS):
+        part = pl.ds(0, chunks * size)
+        return remote(own_hbm.at[part], own.at[part], send_sems.at[n], first_sems.at[0], {"ka": twin})
 
     def tell(r, carry):
         remote(meta_out, meta_in.at[me], meta_sems.at[0], meta_sems.at[1], {"ka": (me + r) % points}).start()
@@ -260,13 +270,16 @@
 
     lax.fori_loop(1, points, tell, 0)
 
-    @pl.when(is_outer)
-    def _():
-        send_own(first, 0, first_sems, hub)
-
-    @pl.when(is_inner)
-    def _():
-        send_own(second, 0, second_sems, hub)
+
+    @pl.when(me == below)
+    def _():
+        send_own(first, 0, first_sems, hub, 0, CHUNKS - 1)
+        send_own(first, 1, first_sems, hub, CHUNKS - 1, CHUNKS)
+
+    @pl.when(me == above)
+    def _():
+        send_own(second, 0, second_sems, hub, 0, CHUNKS - 1)
+        send_own(second, 1, second_sems, hub, CHUNKS - 1, CHUNKS)
 
     corner_low = me == row
     corner_high = me == 2 * row - 1
@@ -284,10 +297,15 @@
     def _():
         send_own(extra, 3, extra_sems, extra_peer)
 
+    @pl.when(corner_low)
+    def _():
+        send_own(extra, 3, extra_sems, extra_peer, 0, EARLY)
+
     @pl.when(is_outer | is_hub)
     def _():
         send_own(first, 2, first_sems, twin)
 
+    map_in.wait()
     indexes, sends, padded = index_tables(map_ref[...], my_slice, slab, capacity)
     tables[...] = jnp.zeros_like(tables)
     for d in range(2):
@@ -340,7 +358,7 @@
     def pick(ref, at):
         return ref[at].reshape(2 * bands, lanes)
 
-    def accumulate(e, c, still, moving, place, inverse, shift):
+    def accumulate(e, c, still, moving, place, inverse, shift, turn=False, count=size):
         line = inverse * shifts + shift
 
         def at(n):
@@ -348,11 +366,13 @@
             return value + jnp.where(value >= slab, place * capacity, 0)
 
         total = sums[e]
-        for u in range(0, size, 2):
-            n = c * size + u
+        for u in range(0, count, 2):
+            n = c * count + u
+            left = jnp.concatenate([pick(still, n), pick(still, n + 1)], axis=1)
+            right = jnp.concatenate([pick(moving, at(n)), pick(moving, at(n + 1))], axis=1)
             total = total + lax.dot_general(
-                jnp.concatenate([pick(still, n), pick(still, n + 1)], axis=1),
-                jnp.concatenate([pick(moving, at(n)), pick(moving, at(n + 1))], axis=1),
+                right if turn else left,
+                left if turn else right,
                 (((1,), (1,)), ((), ())),
                 preferred_element_type=jnp.float32,
             )
@@ -360,10 +380,10 @@
 
     def whole(e, still, moving, place, inverse, shift):
         def step(c, carry):
-            accumulate(e, c, still, moving, place, inverse, shift)
+            accumulate(e, c, still, moving, place, inverse, shift, inverse == 1, LUMP * size)
             return carry
 
-        lax.fori_loop(0, CHUNKS, step, 0)
+        lax.fori_loop(0, CHUNKS // LUMP, step, 0)
 
     def result_copies(e, kind, bra):
         pairs = []
@@ -378,9 +398,10 @@
             pairs.append((at_home, near, away))
         return pairs
 
-    def deliver(e, kind, bra, inverse):
+    def deliver(e, kind, bra, inverse=None):
         total = sums[e]
-        total = jnp.where(inverse == 1, total.T, total)
+        if inverse is not None:
+            total = jnp.where(inverse == 1, total.T, total)
         upper, under = total[:bands], pltpu.roll(total[bands:], bands, 1)
         left = lax.broadcasted_iota(jnp.int32, upper.shape, 1) < bands
         results[e] = upper + jnp.where(left, under, -under)
@@ -397,20 +418,19 @@
         remote(part, part, send_sems.at[0], sems.at[c], {"ka": twin}).wait_recv()
 
     sums[...] = jnp.zeros_like(sums)
-    flip = jnp.where(low, 0, 1)
     extra_inverse = jnp.where(lower_half, 1, 0)
     extra_bra = jnp.where(lower_half, me, me - 1)
     EXTRA = 6
     OWN_EXTRA = 4
-    OUTER_SLOT, INNER_SLOT, CORNER_SLOT = 5, 6, 7
+    BELOW_SLOT, ABOVE_SLOT, CORNER_SLOT = 5, 6, 7
 
     hub_edges = (
-        (first, own, 0, flip, jnp.where(low, outer, hub), ROW),
-        (second, own, 1, 1 - flip, jnp.where(low, hub, inner), ROW),
+        (first, own, 0, 0, below, ROW),
+        (second, own, 1, 1, hub, ROW),
         (third, own, 2, 1, hub, HALF),
         (third, own, 3, 0, far, HALF),
-        (third, first, 0, flip, jnp.where(low, far, outer), ROW),
-        (third, second, 0, 1 - flip, jnp.where(low, inner, far), ROW),
+        (third, first, 0, 0, far, ROW),
+        (third, second, 0, 1, above, ROW),
     )
 
     @pl.when(extra_site)
@@ -438,10 +458,14 @@
             _, _, _, inverse, bra, kind = hub_edges[e]
             offer(e, own, inverse, shift_of(bra, kind))
 
+        def relayed(source, c):
+            return remote(source.at[chunk(c)], first.at[chunk(c)], send_sems.at[4], first_sems.at[c], {"ka": outer})
+
         def relay(c, carry):
             arrived(second, second_sems, c)
-            remote(second.at[chunk(c)], first.at[chunk(c)], send_sems.at[4], first_sems.at[c], {"ka": outer}).start()
+            pl.when(low)(relayed(second, c).start)
             arrived(first, first_sems, c)
+            pl.when(~low)(relayed(first, c).start)
             pl.when(corner_low)(corner_copy(c).start)
             return carry
 
@@ -449,14 +473,14 @@
 
         @pl.when(corner_low)
         def _():
-            send_own(extra, 3, extra_sems, extra_peer)
+            send_own(extra, 3, extra_sems, extra_peer, EARLY, CHUNKS)
 
         @pl.when(corner_high)
         def _():
             sent_own(3).wait_send()
             pl.semaphore_signal(go, inc=1, device_id={"ka": twin}, device_id_type=mesh)
 
-        for n, e in ((OUTER_SLOT, 4), (INNER_SLOT, 5)):
+        for n, e in ((BELOW_SLOT, 4), (ABOVE_SLOT, 5)):
             _, source, _, inverse, bra, kind = hub_edges[e]
             offer(n, source, inverse, shift_of(bra, kind))
 
@@ -468,7 +492,7 @@
             still, moving, place, inverse, bra, kind = hub_edges[e]
             take(e, own, e)
             whole(e, still, moving, place, inverse, shift_of(bra, kind))
-            deliver(e, kind, bra, inverse)
+            deliver(e, kind, bra)
 
         @pl.when(extra_site)
         def _():
@@ -485,8 +509,8 @@
 
         for e in (2, 3):
             take(e, own, e)
-        take(OUTER_SLOT, first, 0)
-        take(INNER_SLOT, second, 0)
+        take(BELOW_SLOT, first, 0)
+        take(ABOVE_SLOT, second, 0)
 
         @pl.when(corner_low)
         def _():
@@ -498,32 +522,41 @@
                 return carry
 
             lax.fori_loop(0, CHUNKS, step, 0)
-            deliver(EXTRA, NEXT, 2 * row - 1, 0)
+            deliver(EXTRA, NEXT, 2 * row - 1)
 
         @pl.when(corner_high)
         def _():
             take(CORNER_SLOT, extra, 0)
+
+        def late_edge(e, c):
+            still, moving, place, inverse, bra, kind = hub_edges[e]
+            accumulate(e, c, still, moving, place, inverse, shift_of(bra, kind), inverse == 1)
+
+        def late_corner(c):
+            accumulate(EXTRA, c, third, extra, 0, 0, shift_of(4 * row - 1, NEXT))
 
         def late(c, carry):
             arrived(third, third_sems, c)
             for e in range(2, 6):
-                still, moving, place, inverse, bra, kind = hub_edges[e]
-                accumulate(e, c, still, moving, place, inverse, shift_of(bra, kind))
+                late_edge(e, c)
 
             @pl.when(corner_high)
             def _():
-                accumulate(EXTRA, c, third, extra, 0, 0, shift_of(4 * row - 1, NEXT))
+                late_corner(c)
 
             return carry
 
-        lax.fori_loop(0, CHUNKS, late, 0)
-        for e in range(2, 6):
-            _, _, _, inverse, bra, kind = hub_edges[e]
-            deliver(e, kind, bra, inverse)
+        lax.fori_loop(0, CHUNKS - 1, late, 0)
+        arrived(third, third_sems, CHUNKS - 1)
 
         @pl.when(corner_high)
         def _():
-            deliver(EXTRA, NEXT, 4 * row - 1, 0)
+            late_corner(CHUNKS - 1)
+            deliver(EXTRA, NEXT, 4 * row - 1)
+
+        for e in (3, 4, 5, 2):
+            late_edge(e, CHUNKS - 1)
+            deliver(e, hub_edges[e][5], hub_edges[e][4])
 
         for e in range(6):
             _, _, _, _, bra, kind = hub_edges[e]
@@ -542,29 +575,30 @@
 
         for e in range(4):
             swap(e).wait_send()
-        swap(OUTER_SLOT).wait_send()
-        swap(INNER_SLOT).wait_send()
+        swap(BELOW_SLOT).wait_send()
+        swap(ABOVE_SLOT).wait_send()
         sent_own(4).wait_send()
 
     @pl.when(is_outer)
     def _():
         for e, inverse, bra in ((0, 1, outer), (1, 0, inner)):
             offer(e, own, inverse, shift_of(bra, HALF))
-        sent_own(0).wait_send()
+        sent_own(0, CHUNKS - 1).wait_send()
         pl.semaphore_signal(go, inc=1, device_id={"ka": twin}, device_id_type=mesh)
         for e in range(2):
             take(e, own, e)
+        pl.when(extra_site & ~lower_half)(extra_edge)
 
         def step(c, carry):
             arrived(first, first_sems, c)
             for e, inverse, bra in ((0, 1, outer), (1, 0, inner)):
-                accumulate(e, c, first, own, e, inverse, shift_of(bra, HALF))
+                accumulate(e, c, first, own, e, inverse, shift_of(bra, HALF), inverse == 1)
             return carry
 
         lax.fori_loop(0, CHUNKS, step, 0)
         for e, inverse, bra in ((0, 1, outer), (1, 0, inner)):
-            deliver(e, HALF, bra, inverse)
-        pl.when(extra_site)(extra_edge)
+            deliver(e, HALF, bra)
+        pl.when(extra_site & lower_half)(extra_edge)
         for e, inverse, bra in ((0, 1, outer), (1, 0, inner)):
             delivered(e, HALF, bra)
             swap(e).wait_send()
@@ -588,7 +622,7 @@
 
         @pl.when(is_inner)
         def _():
-            sent_own(0).wait_send()
+            sent_own(0, CHUNKS - 1).wait_send()
             pl.semaphore_signal(go, inc=1, device_id={"ka": far}, device_id_type=mesh)
 
         @pl.when(gated_extra)
@@ -614,6 +648,10 @@
         delivered(EXTRA, NEXT, extra_bra)
         swap(OWN_EXTRA).wait_send()
 
+    @pl.when(is_outer | is_inner)
+    def _():
+        sent_own(1, 1).wait_send()
+
     @pl.when(is_outer | is_hub)
     def _():
         sent_own(2).wait_send()
@@ -626,9 +664,13 @@
         for g in range(2):
             slot = slots.at[kind, g]
             pltpu.make_async_copy(slot, slot, result_recv.at[kind * 2 + g]).wait()
-        both = slots[kind, 0] + slots[kind, 1]
-        out_ref[kind, 0] = both[:, :bands]
-        out_ref[kind, 1] = both[:, bands:]
+    found = [slots[kind, 0] + slots[kind, 1] for kind in range(ROLES)]
+    for b in range(ROLES):
+        target = near_ref[0, b]
+        chosen = jnp.where(target == (me + row) % points, found[ROW], found[HALF])
+        chosen = jnp.where(target == (me + 1) % points, found[NEXT], chosen)
+        out_ref[b, 0] = chosen[:, :bands]
+        out_ref[b, 1] = chosen[:, bands:]
 
 
 def meet(neighbour, shift_id, block_map, own, points, capacity):
@@ -643,15 +685,13 @@
 
     return pl.pallas_call(
         functools.partial(meet_kernel, points, slab, capacity),
-        out_shape=jax.ShapeDtypeStruct((ROLES, 2, half, bands), jnp.float32),
-        in_specs=[
-            pl.BlockSpec(memory_space=pltpu.SMEM),
-            pl.BlockSpec(memory_space=pltpu.SMEM),
-            pl.BlockSpec(memory_space=pltpu.VMEM),
-            pl.BlockSpec(memory_space=pl.ANY),
-        ],
+        out_shape=pltpu.VMEM((ROLES, 2, half, bands), jnp.float32),
+        in_specs=[pl.BlockSpec(memory_space=pl.ANY)] * 4,
         out_specs=pl.BlockSpec(memory_space=pltpu.VMEM),
         scratch_shapes=[
+            pltpu.SMEM(neighbour.shape, jnp.int32),
+            pltpu.SMEM(shift_id.shape, jnp.int32),
+            pltpu.VMEM(block_map.shape, jnp.int32),
             blocks(slab + 5 * capacity),
             blocks(slab + capacity),
             blocks(slab + 2 * capacity),
@@ -667,7 +707,7 @@
             pltpu.VMEM((ROLES, 2, half, 2 * bands), jnp.float32),
             pltpu.SMEM((points, 1, lanes), jnp.int32),
             pltpu.SMEM((4 * shifts, lanes), jnp.int32),
-            dma((3,)), dma((2,)), dma((6,)),
+            dma((6,)), dma((2,)), dma((6,)),
             dma((CHUNKS,)), dma((CHUNKS,)), dma((CHUNKS,)), dma((CHUNKS,)),
             dma((8,)), dma((8,)), dma((14,)), dma((2 * ROLES,)),
             pltpu.SemaphoreType.REGULAR,
@@ -682,17 +722,8 @@
 def on_four_levels(coeffs, neighbour, shift_id, block_map):
     own = coeffs[0]
     points = lax.axis_size("ka")
-    row = points // 4
-    me = lax.axis_index("ka")
     capacity = 2 * max(1, own.shape[0] // 12)
-    sums = meet(neighbour, shift_id, block_map, own, points, capacity)
-    target = neighbour[0][:, None, None, None]
-    out = jnp.where(
-        target == jnp.mod(me + 1, points),
-        sums[0],
-        jnp.where(target == jnp.mod(me + row, points), sums[1], sums[2]),
-    )
-    return out[None]
+    return meet(neighbour, shift_id, block_map, own, points, capacity)[None]
 
 
 def solution(mesh):

time: 106 us -> 99.2 us (0.936)
  the two profiles are of different devices: /device:TPU:5 before, /device:TPU:1 now
where the time goes in v3:
time: 99.2 us; the launch traced here: 99 us
  Pallas kernels  98.4 us (99%)
    pallas_call x1, Pallas kernels, meet(): pl.pallas_call(functools.partial(meet_kernel, points, slab, capacity), ou...  98.4 us

profile of v3, /device:TPU:1, one launch (start us, length us, event | category | flops | bytes accessed | tf_op | source)
XLA Modules:
  0.0 99.0 jit_solution(13959616469614268260)
XLA Ops:
  0.0 98.4 %meet.1 = f32[3,2,32,64]{3,2,1,0:T(8,128)S(1)} custom-call(s32[1,3]{1,0:T(1,128)} %near_hbm.1, s32[1,3]{1,0:T(1,128)} %shift_hbm.1, s32[8,240]{1,0:T(8,128)} %map_hbm.1, bf16[120,2,64,128]{3,2,1,0:T(8,128)(2,1)} %bitcast.3), custom_call_target="tpu_custom_call" | custom-call | tf_op jit(solution)/shard_map/meet/pallas_call | solution.py:686
  98.4 0.6 copy.6

commit v4 on v3

--- a/solution.py
+++ b/solution.py
@@ -7,9 +7,7 @@
 from jax.experimental import pallas as pl
 from jax.experimental.pallas import tpu as pltpu
 
-CHUNKS = 20
-EARLY = 3
-LUMP = 4
+EARLY = 2
 ROLES = 3
 
 
@@ -181,14 +179,21 @@
     return indexes, sends, padded
 
 
+def pieces(slab):
+    unit = slab // 20
+    sizes = [unit, 3 * unit, 4 * unit, 4 * unit, 4 * unit, 2 * unit, unit, unit - 2, 2]
+    starts = [sum(sizes[:n]) for n in range(len(sizes))]
+    return list(zip(starts, sizes))
+
+
 def meet_kernel(
     points, slab, capacity, near_hbm, shift_hbm, map_hbm, own_hbm, out_ref,
-    near_ref, shift_ref, map_ref, own, first, second, third, extra, packs, landed, meta_out, meta_in, tables,
-    sums, results, slots, meta, table_at,
-    local_sems, meta_sems, send_sems, first_sems, second_sems, third_sems, extra_sems,
-    swap_send, swap_recv, result_send, result_recv, go,
+    near_ref, shift_ref, map_ref, own, first, second, third, extra, packs, landed,
+    meta_out, meta_in, tables, sums, results, slots, meta, table_at,
+    local_sems, meta_send, meta_recv, send_sems, first_sems, second_sems, third_sems, extra_sems,
+    swap_send, swap_recv, result_send, result_recv, go, late_in,
 ):
-    levels = points // (points // 4)
+    levels = 4
     row = points // levels
     me = lax.axis_index("ka")
     my_slice = lax.axis_index("ga")
@@ -206,26 +211,77 @@
     twin = me + 1 - 2 * (column % 2)
     lower_half = z < 2
     bands, lanes = own.shape[2], own.shape[3]
-    size = slab // CHUNKS
     shifts = map_hbm.shape[0]
+    parts = pieces(slab)
+    count = len(parts)
+    tail = parts[count - 2][0]
 
     barrier = pltpu.get_barrier_semaphore()
     mesh = pl.DeviceIdType.MESH
+    is_last = z == levels - 1
 
     def greet(r, carry):
         peer = (me + r) % points
-        for g in range(2):
-            pl.semaphore_signal(barrier, inc=1, device_id={"ka": peer, "ga": g}, device_id_type=mesh)
+
+        @pl.when(~is_last | (peer // row == levels - 1))
+        def _():
+            for g in range(2):
+                pl.semaphore_signal(barrier, inc=1, device_id={"ka": peer, "ga": g}, device_id_type=mesh)
+
         return carry
 
     lax.fori_loop(1, points, greet, 0)
     pl.semaphore_signal(barrier, inc=1, device_id={"ga": partner}, device_id_type=mesh)
-    near_in = pltpu.make_async_copy(near_hbm, near_ref, local_sems.at[3])
-    shift_in = pltpu.make_async_copy(shift_hbm, shift_ref, local_sems.at[4])
-    map_in = pltpu.make_async_copy(map_hbm, map_ref, local_sems.at[5])
-    keep = pltpu.make_async_copy(own_hbm, own.at[pl.ds(0, slab)], local_sems.at[0])
+    near_in = pltpu.make_async_copy(near_hbm, near_ref, local_sems.at[0])
+    shift_in = pltpu.make_async_copy(shift_hbm, shift_ref, local_sems.at[1])
+    map_in = pltpu.make_async_copy(map_hbm, map_ref, local_sems.at[2])
+    keep = pltpu.make_async_copy(own_hbm, own.at[pl.ds(0, slab)], local_sems.at[3])
     for copy in (near_in, shift_in, map_in, keep):
         copy.start()
+    pl.semaphore_wait(barrier, jnp.where(is_last, 2 * points - 1, 2 * (points - row) - 1))
+
+    @pl.when(is_last)
+    def _():
+        def enter(peer, carry):
+            for g in range(2):
+                pl.semaphore_signal(late_in, inc=1, device_id={"ka": peer, "ga": g}, device_id_type=mesh)
+            return carry
+
+        lax.fori_loop(0, points - row, enter, 0)
+
+    def remote(source, target, send, recv, peer):
+        return pltpu.make_async_remote_copy(
+            src_ref=source, dst_ref=target, send_sem=send, recv_sem=recv,
+            device_id=peer, device_id_type=mesh,
+        )
+
+    def chunk(c):
+        return pl.ds(*parts[c])
+
+    def send_own(target, n, sems, peer, start=0, stop=count):
+        for c in range(start, stop):
+            remote(own_hbm.at[chunk(c)], target.at[chunk(c)], send_sems.at[n], sems.at[c], {"ka": peer}).start()
+
+    def sent_own(n, size=slab):
+        part = pl.ds(0, size)
+        return remote(own_hbm.at[part], own.at[part], send_sems.at[n], first_sems.at[0], {"ka": twin})
+
+    def arrived(buffer, sems, c):
+        part = buffer.at[chunk(c)]
+        remote(part, part, send_sems.at[0], sems.at[c], {"ka": twin}).wait_recv()
+
+    def main_sends(pairs):
+        @pl.when(me == below)
+        def _():
+            for n, start, stop in pairs:
+                send_own(first, n, first_sems, hub, start, stop)
+
+        @pl.when(me == above)
+        def _():
+            for n, start, stop in pairs:
+                send_own(second, n, second_sems, hub, start, stop)
+
+    main_sends(((0, 0, 1),))
     near_in.wait()
     shift_in.wait()
 
@@ -242,51 +298,36 @@
     )
     meta_out[...] = facts
     meta_in[me] = facts
-    pl.semaphore_wait(barrier, 2 * points - 1)
-
-    def remote(source, target, send, recv, peer):
-        return pltpu.make_async_remote_copy(
-            src_ref=source, dst_ref=target, send_sem=send, recv_sem=recv,
-            device_id=peer, device_id_type=mesh,
-        )
-
-    def chunk(c):
-        return pl.ds(c * size, size)
-
-    def own_part(c, target, n, sems, peer):
-        return remote(own_hbm.at[chunk(c)], target.at[chunk(c)], send_sems.at[n], sems.at[c], {"ka": peer})
-
-    def send_own(target, n, sems, peer, start=0, stop=CHUNKS):
-        for c in range(start, stop):
-            own_part(c, target, n, sems, peer).start()
-
-    def sent_own(n, chunks=CHUNKS):
-        part = pl.ds(0, chunks * size)
-        return remote(own_hbm.at[part], own.at[part], send_sems.at[n], first_sems.at[0], {"ka": twin})
-
-    def tell(r, carry):
-        remote(meta_out, meta_in.at[me], meta_sems.at[0], meta_sems.at[1], {"ka": (me + r) % points}).start()
-        return carry
-
-    lax.fori_loop(1, points, tell, 0)
-
-
-    @pl.when(me == below)
-    def _():
-        send_own(first, 0, first_sems, hub, 0, CHUNKS - 1)
-        send_own(first, 1, first_sems, hub, CHUNKS - 1, CHUNKS)
-
-    @pl.when(me == above)
-    def _():
-        send_own(second, 0, second_sems, hub, 0, CHUNKS - 1)
-        send_own(second, 1, second_sems, hub, CHUNKS - 1, CHUNKS)
+
+    @pl.when(~is_last)
+    def _():
+        pl.semaphore_wait(late_in, 2 * row)
+
+    notices = (
+        (~is_hub, hub),
+        (is_inner, outer),
+        (me == me, twin),
+        ((z >= 2) & (column % 2 == 1) & (me != points - 1), me + 1),
+        (me == 2 * row - 1, row),
+    )
+    heard = (
+        (is_hub, 0, 3), (is_outer, 1, 1), (me == me, 2, 1),
+        ((z >= 2) & (column % 2 == 0) & (me != 2 * row), 3, 1), (me == row, 4, 1),
+    )
+
+    def notice(n, peer):
+        return remote(meta_out, meta_in.at[me], meta_send.at[n], meta_recv.at[n], {"ka": peer})
+
+    for n, (sends, peer) in enumerate(notices):
+        pl.when(sends)(notice(n, peer).start)
+
+    main_sends(((0, 1, count - 2), (1, count - 2, count)))
 
     corner_low = me == row
     corner_high = me == 2 * row - 1
-    gated_extra = me == row + 2
-    extra_down = me == 2
+    extra_down = (me == 2) | (me == row + 2)
     extra_up = (me == 2 * row + 1) | (me == 2 * row + 3) | (me == 3 * row + 1)
-    extra_source = extra_down | extra_up | corner_low | gated_extra
+    extra_source = extra_down | extra_up | corner_low | corner_high
     extra_site = (
         (me == row - 1) | (me == 1) | (me == row + 1)
         | (me == 2 * row + 2) | (me == 3 * row) | (me == 3 * row + 2)
@@ -311,15 +352,37 @@
     for d in range(2):
         tables[pl.ds(d * shifts, shifts), pl.ds(0, slab)] = indexes[d]
         tables[pl.ds((2 + d) * shifts, shifts), pl.ds(0, padded)] = sends[d]
-
-    told = meta_in.at[pl.ds(0, points - 1)]
-    all_told = remote(told, told, meta_sems.at[0], meta_sems.at[1], {"ka": twin})
-    tables_in = pltpu.make_async_copy(tables, table_at, local_sems.at[1])
+    tables_in = pltpu.make_async_copy(tables, table_at, local_sems.at[0])
     tables_in.start()
-    all_told.wait_recv()
-    meta_copy = pltpu.make_async_copy(meta_in, meta, local_sems.at[2])
+
+    def corner_copy(c):
+        return remote(first.at[chunk(c)], extra.at[chunk(c)], send_sems.at[5], extra_sems.at[c], {"ka": 2 * row - 1})
+
+    def relayed(source, c):
+        return remote(source.at[chunk(c)], first.at[chunk(c)], send_sems.at[4], first_sems.at[c], {"ka": outer})
+
+    def relay(c):
+        arrived(second, second_sems, c)
+        pl.when(low)(relayed(second, c).start)
+        arrived(first, first_sems, c)
+        pl.when(~low)(relayed(first, c).start)
+        pl.when(corner_low)(corner_copy(c).start)
+
+    @pl.when(is_hub)
+    def _():
+        relay(0)
+
+    for hears, n, amount in heard:
+
+        @pl.when(hears)
+        def _():
+            fact = meta_in.at[pl.ds(0, amount)]
+            remote(fact, fact, meta_send.at[0], meta_recv.at[n], {"ka": twin}).wait_recv()
+
+    meta_copy = pltpu.make_async_copy(meta_in, meta, local_sems.at[1])
     meta_copy.start()
-    all_told.wait_send()
+    for n, (sends, peer) in enumerate(notices):
+        pl.when(sends)(notice(n, peer).wait_send)
     meta_copy.wait()
     tables_in.wait()
     keep.wait()
@@ -328,21 +391,26 @@
         return meta[point, 0, kind]
 
     NEXT, ROW, HALF = 0, 1, 2
-
-    def swap(n):
-        part = pl.ds(n * capacity, capacity)
-        return remote(packs.at[part], landed.at[part], swap_send.at[n], swap_recv.at[n], {"ga": partner})
-
-    def take(n, target, place):
-        swap(n).wait_recv()
-
+    OWN_EXTRA, BELOW_SLOT, ABOVE_SLOT, CORNER_SLOT = 4, 5, 6, 7
+    groups = (0, 0, 0, 0, 1, 2, 2, 3)
+
+    def swap(n, many=1):
+        part = pl.ds(n * capacity, many * capacity)
+        group = groups[n]
+        return remote(packs.at[part], landed.at[part], swap_send.at[group], swap_recv.at[group], {"ga": partner})
+
+    def place_landed(n, target, place):
         def move(r, carry):
             target[slab + place * capacity + r] = landed[n * capacity + r]
             return carry
 
         lax.fori_loop(0, capacity, move, 0, unroll=4)
 
-    def pack(n, source, inverse, shift):
+    def take(n, target, place):
+        swap(n).wait_recv()
+        place_landed(n, target, place)
+
+    def offer(n, source, inverse, shift):
         line = (2 + inverse) * shifts + shift
 
         def gather(r, carry):
@@ -350,79 +418,78 @@
             return carry
 
         lax.fori_loop(0, capacity, gather, 0, unroll=4)
-
-    def offer(n, source, inverse, shift):
-        pack(n, source, inverse, shift)
         swap(n).start()
 
     def pick(ref, at):
         return ref[at].reshape(2 * bands, lanes)
 
-    def accumulate(e, c, still, moving, place, inverse, shift, turn=False, count=size):
+    def accumulate(e, part, still, moving, place, inverse, shift, turn=False):
+        start, size = part
         line = inverse * shifts + shift
 
         def at(n):
             value = table_at[line, n]
             return value + jnp.where(value >= slab, place * capacity, 0)
 
-        total = sums[e]
-        for u in range(0, count, 2):
-            n = c * count + u
-            left = jnp.concatenate([pick(still, n), pick(still, n + 1)], axis=1)
-            right = jnp.concatenate([pick(moving, at(n)), pick(moving, at(n + 1))], axis=1)
-            total = total + lax.dot_general(
-                right if turn else left,
-                left if turn else right,
-                (((1,), (1,)), ((), ())),
-                preferred_element_type=jnp.float32,
+        def products(begin, many, total):
+            for u in range(0, many, 2):
+                n = begin + u
+                left = jnp.concatenate([pick(still, n), pick(still, n + 1)], axis=1)
+                right = jnp.concatenate([pick(moving, at(n)), pick(moving, at(n + 1))], axis=1)
+                total = total + lax.dot_general(
+                    right if turn else left,
+                    left if turn else right,
+                    (((1,), (1,)), ((), ())),
+                    preferred_element_type=jnp.float32,
+                )
+            return total
+
+        steps = [s for s in (12, 6, 4, 2) if size % s == 0][0]
+        if steps == size:
+            sums[e] = products(start, size, sums[e])
+        else:
+            sums[e] = lax.fori_loop(
+                0, size // steps, lambda i, total: products(start + i * steps, steps, total), sums[e]
             )
-        sums[e] = total
-
-    def whole(e, still, moving, place, inverse, shift):
-        def step(c, carry):
-            accumulate(e, c, still, moving, place, inverse, shift, inverse == 1, LUMP * size)
-            return carry
-
-        lax.fori_loop(0, CHUNKS // LUMP, step, 0)
-
-    def result_copies(e, kind, bra):
-        pairs = []
+
+    def result_copies(e, kind, bra, base):
+        copies = []
         half = bands // 2
         for g in range(2):
             source = results.at[e, pl.ds(g * half, half)]
             target = slots.at[kind, my_slice]
-            arrived = result_recv.at[kind * 2 + my_slice]
             at_home = (bra == me) & (my_slice == g)
-            near = pltpu.make_async_copy(source, target, arrived)
-            away = remote(source, target, result_send.at[e * 2 + g], arrived, {"ka": bra, "ga": g})
-            pairs.append((at_home, near, away))
-        return pairs
-
-    def deliver(e, kind, bra, inverse=None):
+            near = pltpu.make_async_copy(source, target, result_recv.at[0])
+            send = 0 if base is None else base + g
+            away = remote(source, target, result_send.at[send], result_recv.at[0], {"ka": bra, "ga": g})
+            copies.append((at_home, near, away))
+        return copies
+
+    def settle(e, inverse=None):
         total = sums[e]
         if inverse is not None:
             total = jnp.where(inverse == 1, total.T, total)
         upper, under = total[:bands], pltpu.roll(total[bands:], bands, 1)
         left = lax.broadcasted_iota(jnp.int32, upper.shape, 1) < bands
         results[e] = upper + jnp.where(left, under, -under)
-        for at_home, near, away in result_copies(e, kind, bra):
+
+    def dispatch(e, kind, bra, base):
+        for at_home, near, away in result_copies(e, kind, bra, base):
             pl.when(at_home)(near.start)
             pl.when(~at_home)(away.start)
 
-    def delivered(e, kind, bra):
-        for at_home, _, away in result_copies(e, kind, bra):
+    def deliver(e, kind, bra, base, inverse=None):
+        settle(e, inverse)
+        dispatch(e, kind, bra, base)
+
+    def delivered(e, kind, bra, base):
+        for at_home, _, away in result_copies(e, kind, bra, base):
             pl.when(~at_home)(away.wait_send)
-
-    def arrived(buffer, sems, c):
-        part = buffer.at[chunk(c)]
-        remote(part, part, send_sems.at[0], sems.at[c], {"ka": twin}).wait_recv()
 
     sums[...] = jnp.zeros_like(sums)
     extra_inverse = jnp.where(lower_half, 1, 0)
     extra_bra = jnp.where(lower_half, me, me - 1)
-    EXTRA = 6
-    OWN_EXTRA = 4
-    BELOW_SLOT, ABOVE_SLOT, CORNER_SLOT = 5, 6, 7
+    EXTRA, EXTRA_BASE = 6, 4
 
     hub_edges = (
         (first, own, 0, 0, below, ROW),
@@ -440,17 +507,10 @@
     def extra_edge():
         take(OWN_EXTRA, own, OWN_EXTRA)
         shift = shift_of(extra_bra, NEXT)
-
-        def step(c, carry):
+        for c in range(count):
             arrived(extra, extra_sems, c)
-            accumulate(EXTRA, c, extra, own, OWN_EXTRA, extra_inverse, shift)
-            return carry
-
-        lax.fori_loop(0, CHUNKS, step, 0)
-        deliver(EXTRA, NEXT, extra_bra, extra_inverse)
-
-    def corner_copy(c):
-        return remote(first.at[chunk(c)], extra.at[chunk(c)], send_sems.at[5], extra_sems.at[c], {"ka": 2 * row - 1})
+            accumulate(EXTRA, parts[c], extra, own, OWN_EXTRA, extra_inverse, shift)
+        deliver(EXTRA, NEXT, extra_bra, EXTRA_BASE, extra_inverse)
 
     @pl.when(is_hub)
     def _():
@@ -458,27 +518,12 @@
             _, _, _, inverse, bra, kind = hub_edges[e]
             offer(e, own, inverse, shift_of(bra, kind))
 
-        def relayed(source, c):
-            return remote(source.at[chunk(c)], first.at[chunk(c)], send_sems.at[4], first_sems.at[c], {"ka": outer})
-
-        def relay(c, carry):
-            arrived(second, second_sems, c)
-            pl.when(low)(relayed(second, c).start)
-            arrived(first, first_sems, c)
-            pl.when(~low)(relayed(first, c).start)
-            pl.when(corner_low)(corner_copy(c).start)
-            return carry
-
-        lax.fori_loop(0, CHUNKS, relay, 0)
+        for c in range(1, count):
+            relay(c)
 
         @pl.when(corner_low)
         def _():
-            send_own(extra, 3, extra_sems, extra_peer, EARLY, CHUNKS)
-
-        @pl.when(corner_high)
-        def _():
-            sent_own(3).wait_send()
-            pl.semaphore_signal(go, inc=1, device_id={"ka": twin}, device_id_type=mesh)
+            send_own(extra, 3, extra_sems, extra_peer, EARLY, count)
 
         for n, e in ((BELOW_SLOT, 4), (ABOVE_SLOT, 5)):
             _, source, _, inverse, bra, kind = hub_edges[e]
@@ -488,11 +533,13 @@
         def _():
             offer(CORNER_SLOT, second, 0, shift_of(2 * row - 1, NEXT))
 
+        swap(0, 4).wait_recv()
+        for e in range(4):
+            place_landed(e, own, e)
         for e in range(2):
             still, moving, place, inverse, bra, kind = hub_edges[e]
-            take(e, own, e)
-            whole(e, still, moving, place, inverse, shift_of(bra, kind))
-            deliver(e, kind, bra)
+            accumulate(e, (0, slab), still, moving, place, inverse, shift_of(bra, kind), inverse == 1)
+            deliver(e, kind, bra, None)
 
         @pl.when(extra_site)
         def _():
@@ -500,108 +547,87 @@
 
         @pl.when(corner_high)
         def _():
-            def gain(c, carry):
+            for c in range(count):
                 arrived(extra, extra_sems, c)
-                return carry
-
-            lax.fori_loop(0, CHUNKS, gain, 0)
             offer(CORNER_SLOT, extra, 0, shift_of(4 * row - 1, NEXT))
 
-        for e in (2, 3):
-            take(e, own, e)
-        take(BELOW_SLOT, first, 0)
-        take(ABOVE_SLOT, second, 0)
+        swap(BELOW_SLOT, 2).wait_recv()
+        place_landed(BELOW_SLOT, first, 0)
+        place_landed(ABOVE_SLOT, second, 0)
 
         @pl.when(corner_low)
         def _():
             take(CORNER_SLOT, second, 1)
 
-            def step(c, carry):
+        @pl.when(corner_high)
+        def _():
+            take(CORNER_SLOT, extra, 0)
+
+        for c in range(count):
+            arrived(third, third_sems, c)
+
+            @pl.when(corner_low)
+            def _():
                 arrived(extra, extra_sems, c)
-                accumulate(EXTRA, c, extra, second, 1, 0, shift_of(2 * row - 1, NEXT))
-                return carry
-
-            lax.fori_loop(0, CHUNKS, step, 0)
-            deliver(EXTRA, NEXT, 2 * row - 1)
-
-        @pl.when(corner_high)
-        def _():
-            take(CORNER_SLOT, extra, 0)
-
-        def late_edge(e, c):
-            still, moving, place, inverse, bra, kind = hub_edges[e]
-            accumulate(e, c, still, moving, place, inverse, shift_of(bra, kind), inverse == 1)
-
-        def late_corner(c):
-            accumulate(EXTRA, c, third, extra, 0, 0, shift_of(4 * row - 1, NEXT))
-
-        def late(c, carry):
-            arrived(third, third_sems, c)
-            for e in range(2, 6):
-                late_edge(e, c)
+                accumulate(EXTRA, parts[c], extra, second, 1, 0, shift_of(2 * row - 1, NEXT))
+                if c == count - 1:
+                    deliver(EXTRA, NEXT, 2 * row - 1, EXTRA_BASE)
 
             @pl.when(corner_high)
             def _():
-                late_corner(c)
-
-            return carry
-
-        lax.fori_loop(0, CHUNKS - 1, late, 0)
-        arrived(third, third_sems, CHUNKS - 1)
-
-        @pl.when(corner_high)
-        def _():
-            late_corner(CHUNKS - 1)
-            deliver(EXTRA, NEXT, 4 * row - 1)
+                accumulate(EXTRA, parts[c], third, extra, 0, 0, shift_of(4 * row - 1, NEXT))
+                if c == count - 1:
+                    deliver(EXTRA, NEXT, 4 * row - 1, EXTRA_BASE)
+
+            for e in (3, 4, 5, 2):
+                still, moving, place, inverse, bra, kind = hub_edges[e]
+                accumulate(e, parts[c], still, moving, place, inverse, shift_of(bra, kind), inverse == 1)
 
         for e in (3, 4, 5, 2):
-            late_edge(e, CHUNKS - 1)
-            deliver(e, hub_edges[e][5], hub_edges[e][4])
-
-        for e in range(6):
-            _, _, _, _, bra, kind = hub_edges[e]
-            delivered(e, kind, bra)
+            settle(e)
+        for e in (3, 4, 5, 2):
+            dispatch(e, hub_edges[e][5], hub_edges[e][4], None)
+
+        sent = results.at[pl.ds(0, 5)]
+        remote(sent, sent, result_send.at[0], result_recv.at[0], {"ka": twin}).wait_send()
 
         @pl.when(corner_low)
         def _():
-            delivered(EXTRA, NEXT, 2 * row - 1)
+            delivered(EXTRA, NEXT, 2 * row - 1, EXTRA_BASE)
             swap(CORNER_SLOT).wait_send()
             sent_own(5).wait_send()
 
         @pl.when(corner_high)
         def _():
-            delivered(EXTRA, NEXT, 4 * row - 1)
+            delivered(EXTRA, NEXT, 4 * row - 1, EXTRA_BASE)
             swap(CORNER_SLOT).wait_send()
 
-        for e in range(4):
-            swap(e).wait_send()
-        swap(BELOW_SLOT).wait_send()
-        swap(ABOVE_SLOT).wait_send()
+        swap(0, 4).wait_send()
+        swap(BELOW_SLOT, 2).wait_send()
         sent_own(4).wait_send()
 
+    outer_edges = ((0, 1, outer), (1, 0, inner))
+
     @pl.when(is_outer)
     def _():
-        for e, inverse, bra in ((0, 1, outer), (1, 0, inner)):
+        for e, inverse, bra in outer_edges:
             offer(e, own, inverse, shift_of(bra, HALF))
-        sent_own(0, CHUNKS - 1).wait_send()
+        sent_own(0, tail).wait_send()
         pl.semaphore_signal(go, inc=1, device_id={"ka": twin}, device_id_type=mesh)
+        swap(0, 2).wait_recv()
         for e in range(2):
-            take(e, own, e)
+            place_landed(e, own, e)
         pl.when(extra_site & ~lower_half)(extra_edge)
-
-        def step(c, carry):
+        for c in range(count):
             arrived(first, first_sems, c)
-            for e, inverse, bra in ((0, 1, outer), (1, 0, inner)):
-                accumulate(e, c, first, own, e, inverse, shift_of(bra, HALF), inverse == 1)
-            return carry
-
-        lax.fori_loop(0, CHUNKS, step, 0)
-        for e, inverse, bra in ((0, 1, outer), (1, 0, inner)):
-            deliver(e, HALF, bra)
+            for e, inverse, bra in outer_edges:
+                accumulate(e, parts[c], first, own, e, inverse, shift_of(bra, HALF), inverse == 1)
+        for e, inverse, bra in outer_edges:
+            deliver(e, HALF, bra, 2 * e)
         pl.when(extra_site & lower_half)(extra_edge)
-        for e, inverse, bra in ((0, 1, outer), (1, 0, inner)):
-            delivered(e, HALF, bra)
-            swap(e).wait_send()
+        for e, inverse, bra in outer_edges:
+            delivered(e, HALF, bra, 2 * e)
+        swap(0, 2).wait_send()
 
     twin_inverse = jnp.where(column % 2 == 1, 0, 1)
     twin_bra = me - column % 2
@@ -611,46 +637,34 @@
         shift = shift_of(twin_bra, NEXT)
         offer(0, own, twin_inverse, shift)
         take(0, own, 0)
-
-        def step(c, carry):
+        for c in range(count):
             arrived(first, first_sems, c)
-            accumulate(0, c, first, own, 0, twin_inverse, shift)
-            return carry
-
-        lax.fori_loop(0, CHUNKS, step, 0)
-        deliver(0, NEXT, twin_bra, twin_inverse)
+        accumulate(0, (0, slab), first, own, 0, twin_inverse, shift)
+        deliver(0, NEXT, twin_bra, 0, twin_inverse)
 
         @pl.when(is_inner)
         def _():
-            sent_own(0, CHUNKS - 1).wait_send()
+            sent_own(0, tail).wait_send()
             pl.semaphore_signal(go, inc=1, device_id={"ka": far}, device_id_type=mesh)
-
-        @pl.when(gated_extra)
-        def _():
-            pl.semaphore_wait(go, 1)
 
         @pl.when(is_far)
         def _():
             pl.semaphore_wait(go, 2)
             send_own(third, 0, third_sems, hub)
 
-        @pl.when(gated_extra)
-        def _():
-            send_own(extra, 3, extra_sems, extra_peer)
-
         pl.when(extra_site)(extra_edge)
-        delivered(0, NEXT, twin_bra)
+        delivered(0, NEXT, twin_bra, 0)
         swap(0).wait_send()
         pl.when(is_far)(sent_own(0).wait_send)
 
     @pl.when(extra_site)
     def _():
-        delivered(EXTRA, NEXT, extra_bra)
+        delivered(EXTRA, NEXT, extra_bra, EXTRA_BASE)
         swap(OWN_EXTRA).wait_send()
 
     @pl.when(is_outer | is_inner)
     def _():
-        sent_own(1, 1).wait_send()
+        sent_own(1, slab - tail).wait_send()
 
     @pl.when(is_outer | is_hub)
     def _():
@@ -660,10 +674,7 @@
     def _():
         sent_own(3).wait_send()
 
-    for kind in range(ROLES):
-        for g in range(2):
-            slot = slots.at[kind, g]
-            pltpu.make_async_copy(slot, slot, result_recv.at[kind * 2 + g]).wait()
+    pltpu.make_async_copy(slots, slots, result_recv.at[0]).wait()
     found = [slots[kind, 0] + slots[kind, 1] for kind in range(ROLES)]
     for b in range(ROLES):
         target = near_ref[0, b]
@@ -679,6 +690,7 @@
     shifts = block_map.shape[0]
     half = bands // 2
     dma = pltpu.SemaphoreType.DMA
+    flows = len(pieces(slab))
 
     def blocks(count):
         return pltpu.VMEM((count,) + block, own.dtype)
@@ -707,9 +719,10 @@
             pltpu.VMEM((ROLES, 2, half, 2 * bands), jnp.float32),
             pltpu.SMEM((points, 1, lanes), jnp.int32),
             pltpu.SMEM((4 * shifts, lanes), jnp.int32),
-            dma((6,)), dma((2,)), dma((6,)),
-            dma((CHUNKS,)), dma((CHUNKS,)), dma((CHUNKS,)), dma((CHUNKS,)),
-            dma((8,)), dma((8,)), dma((14,)), dma((2 * ROLES,)),
+            dma((4,)), dma((5,)), dma((5,)), dma((6,)),
+            dma((flows,)), dma((flows,)), dma((flows,)), dma((flows,)),
+            dma((4,)), dma((4,)), dma((6,)), dma((1,)),
+            pltpu.SemaphoreType.REGULAR,
             pltpu.SemaphoreType.REGULAR,
         ],
         compiler_params=pltpu.CompilerParams(
@@ -736,7 +749,7 @@
         one_each = coeffs.shape[0] == mesh.shape["ka"] and neighbour.shape[1] == ROLES
         per_slice = coeffs.shape[1] // mesh.shape["ga"]
         lanes = coeffs.shape[4]
-        fits = per_slice % (2 * CHUNKS) == 0 and per_slice <= lanes and 2 * coeffs.shape[3] == lanes
+        fits = per_slice % 40 == 0 and 80 <= per_slice <= lanes and 2 * coeffs.shape[3] == lanes
         body = on_four_levels if square and one_each and fits else on_device
         return jax.shard_map(
             body, mesh=mesh, in_specs=in_specs, out_specs=out_specs, check_vma=False

time: 99.2 us -> 98 us (0.988)
  the two profiles are of different devices: /device:TPU:1 before, /device:TPU:5 now
where the time goes in v4:
time: 98 us; the launch traced here: 96.9 us
  Pallas kernels  96.2 us (98%)
    pallas_call x1, Pallas kernels, meet(): pl.pallas_call(functools.partial(meet_kernel, points, slab, capacity), ou...  96.2 us

profile of v4, /device:TPU:5, one launch (start us, length us, event | category | flops | bytes accessed | tf_op | source)
XLA Modules:
  0.0 96.9 jit_solution(8246432365552405630)
XLA Ops:
  0.0 96.2 %meet.1 = f32[3,2,32,64]{3,2,1,0:T(8,128)S(1)} custom-call(s32[1,3]{1,0:T(1,128)} %near_hbm.1, s32[1,3]{1,0:T(1,128)} %shift_hbm.1, s32[8,240]{1,0:T(8,128)} %map_hbm.1, bf16[120,2,64,128]{3,2,1,0:T(8,128)(2,1)} %bitcast.3), custom_call_target="tpu_custom_call" | custom-call | tf_op jit(solution)/shard_map/meet/pallas_call | solution.py:698
  96.2 0.6 copy.6

commit v5 on v4

--- a/solution.py
+++ b/solution.py
@@ -8,6 +8,7 @@
 from jax.experimental.pallas import tpu as pltpu
 
 EARLY = 2
+MIDDLE = 4
 ROLES = 3
 
 
@@ -218,36 +219,49 @@
 
     barrier = pltpu.get_barrier_semaphore()
     mesh = pl.DeviceIdType.MESH
-    is_last = z == levels - 1
-
-    def greet(r, carry):
-        peer = (me + r) % points
-
-        @pl.when(~is_last | (peer // row == levels - 1))
-        def _():
-            for g in range(2):
-                pl.semaphore_signal(barrier, inc=1, device_id={"ka": peer, "ga": g}, device_id_type=mesh)
-
-        return carry
-
-    lax.fori_loop(1, points, greet, 0)
-    pl.semaphore_signal(barrier, inc=1, device_id={"ga": partner}, device_id_type=mesh)
+    corner_low = me == row
+    corner_high = me == 2 * row - 1
+    high_source = me == 3 * row - 1
+    high_site = me == 3 * row
+
+    def signal(semaphore, peer):
+        pl.semaphore_signal(semaphore, inc=1, device_id=peer, device_id_type=mesh)
+
+    signal(barrier, {"ga": partner})
+    signal(barrier, {"ka": twin})
+    greetings = (
+        (~is_hub, hub), (is_hub, outer), (is_hub, inner), (is_hub | is_inner, far),
+        (column == 1, me + 1), (column == 2, me - 1), (me == row - 1, row), (corner_low, row - 1),
+        (corner_low, 2 * row - 1), (corner_high, row), (high_source, 3 * row),
+    )
+    for greets, peer in greetings:
+
+        @pl.when(greets)
+        def _():
+            signal(barrier, {"ka": peer})
+
+    expected = (
+        (is_hub, 3), (~is_hub, 1), (is_far, 1), ((column == 1) | (column == 2), 1),
+        (me == row - 1, 1), (corner_low, 2), (corner_high, 1), (high_site, 1),
+    )
+    greeted = jnp.int32(2)
+    for hears, amount in expected:
+        greeted = greeted + jnp.where(hears, amount, 0)
     near_in = pltpu.make_async_copy(near_hbm, near_ref, local_sems.at[0])
     shift_in = pltpu.make_async_copy(shift_hbm, shift_ref, local_sems.at[1])
     map_in = pltpu.make_async_copy(map_hbm, map_ref, local_sems.at[2])
     keep = pltpu.make_async_copy(own_hbm, own.at[pl.ds(0, slab)], local_sems.at[3])
     for copy in (near_in, shift_in, map_in, keep):
         copy.start()
-    pl.semaphore_wait(barrier, jnp.where(is_last, 2 * points - 1, 2 * (points - row) - 1))
-
-    @pl.when(is_last)
-    def _():
-        def enter(peer, carry):
-            for g in range(2):
-                pl.semaphore_signal(late_in, inc=1, device_id={"ka": peer, "ga": g}, device_id_type=mesh)
-            return carry
-
-        lax.fori_loop(0, points - row, enter, 0)
+    pl.semaphore_wait(barrier, greeted)
+
+    @pl.when(is_far)
+    def _():
+        signal(late_in, {"ka": inner})
+
+    @pl.when(high_site)
+    def _():
+        signal(late_in, {"ka": me - 1})
 
     def remote(source, target, send, recv, peer):
         return pltpu.make_async_remote_copy(
@@ -299,32 +313,34 @@
     meta_out[...] = facts
     meta_in[me] = facts
 
-    @pl.when(~is_last)
-    def _():
-        pl.semaphore_wait(late_in, 2 * row)
-
+    steps_up = (z >= 2) & (column % 2 == 1) & (me != points - 1)
     notices = (
         (~is_hub, hub),
-        (is_inner, outer),
+        (is_hub, outer),
         (me == me, twin),
-        ((z >= 2) & (column % 2 == 1) & (me != points - 1), me + 1),
-        (me == 2 * row - 1, row),
+        (steps_up, me + 1),
+        (corner_high, row),
     )
     heard = (
         (is_hub, 0, 3), (is_outer, 1, 1), (me == me, 2, 1),
-        ((z >= 2) & (column % 2 == 0) & (me != 2 * row), 3, 1), (me == row, 4, 1),
+        ((z >= 2) & (column % 2 == 0) & (me != 2 * row), 3, 1), (corner_low, 4, 1),
     )
 
     def notice(n, peer):
-        return remote(meta_out, meta_in.at[me], meta_send.at[n], meta_recv.at[n], {"ka": peer})
-
-    for n, (sends, peer) in enumerate(notices):
-        pl.when(sends)(notice(n, peer).start)
+        source = meta_out if n != 1 else meta_in.at[inner]
+        target = meta_in.at[me] if n != 1 else meta_in.at[inner]
+        return remote(source, target, meta_send.at[n], meta_recv.at[n], {"ka": peer})
+
+    for n in (0, 2, 4):
+        pl.when(notices[n][0])(notice(n, notices[n][1]).start)
 
     main_sends(((0, 1, count - 2), (1, count - 2, count)))
 
-    corner_low = me == row
-    corner_high = me == 2 * row - 1
+    @pl.when(high_source)
+    def _():
+        pl.semaphore_wait(late_in, 2)
+
+    pl.when(steps_up)(notice(3, me + 1).start)
     extra_down = (me == 2) | (me == row + 2)
     extra_up = (me == 2 * row + 1) | (me == 2 * row + 3) | (me == 3 * row + 1)
     extra_source = extra_down | extra_up | corner_low | corner_high
@@ -378,11 +394,11 @@
         def _():
             fact = meta_in.at[pl.ds(0, amount)]
             remote(fact, fact, meta_send.at[0], meta_recv.at[n], {"ka": twin}).wait_recv()
+            if n == 0:
+                notice(1, outer).start()
 
     meta_copy = pltpu.make_async_copy(meta_in, meta, local_sems.at[1])
     meta_copy.start()
-    for n, (sends, peer) in enumerate(notices):
-        pl.when(sends)(notice(n, peer).wait_send)
     meta_copy.wait()
     tables_in.wait()
     keep.wait()
@@ -455,12 +471,12 @@
     def result_copies(e, kind, bra, base):
         copies = []
         half = bands // 2
-        for g in range(2):
+        for n, g in enumerate((partner, my_slice)):
             source = results.at[e, pl.ds(g * half, half)]
             target = slots.at[kind, my_slice]
-            at_home = (bra == me) & (my_slice == g)
+            at_home = bra == me
             near = pltpu.make_async_copy(source, target, result_recv.at[0])
-            send = 0 if base is None else base + g
+            send = 0 if base is None else base + n
             away = remote(source, target, result_send.at[send], result_recv.at[0], {"ka": bra, "ga": g})
             copies.append((at_home, near, away))
         return copies
@@ -473,18 +489,24 @@
         left = lax.broadcasted_iota(jnp.int32, upper.shape, 1) < bands
         results[e] = upper + jnp.where(left, under, -under)
 
-    def dispatch(e, kind, bra, base):
-        for at_home, near, away in result_copies(e, kind, bra, base):
-            pl.when(at_home)(near.start)
-            pl.when(~at_home)(away.start)
+    def dispatch(edges, base):
+        for n in range(2):
+            for e, kind, bra in edges:
+                at_home, near, away = result_copies(e, kind, bra, base)[n]
+                if n == 0:
+                    away.start()
+                else:
+                    pl.when(at_home)(near.start)
+                    pl.when(~at_home)(away.start)
 
     def deliver(e, kind, bra, base, inverse=None):
         settle(e, inverse)
-        dispatch(e, kind, bra, base)
+        dispatch(((e, kind, bra),), base)
 
     def delivered(e, kind, bra, base):
-        for at_home, _, away in result_copies(e, kind, bra, base):
-            pl.when(~at_home)(away.wait_send)
+        first_copy, second_copy = result_copies(e, kind, bra, base)
+        first_copy[2].wait_send()
+        pl.when(~second_copy[0])(second_copy[2].wait_send)
 
     sums[...] = jnp.zeros_like(sums)
     extra_inverse = jnp.where(lower_half, 1, 0)
@@ -523,7 +545,7 @@
 
         @pl.when(corner_low)
         def _():
-            send_own(extra, 3, extra_sems, extra_peer, EARLY, count)
+            send_own(extra, 3, extra_sems, extra_peer, EARLY, MIDDLE)
 
         for n, e in ((BELOW_SLOT, 4), (ABOVE_SLOT, 5)):
             _, source, _, inverse, bra, kind = hub_edges[e]
@@ -541,6 +563,10 @@
             accumulate(e, (0, slab), still, moving, place, inverse, shift_of(bra, kind), inverse == 1)
             deliver(e, kind, bra, None)
 
+        @pl.when(corner_low)
+        def _():
+            send_own(extra, 3, extra_sems, extra_peer, MIDDLE, count)
+
         @pl.when(extra_site)
         def _():
             extra_edge()
@@ -585,8 +611,7 @@
 
         for e in (3, 4, 5, 2):
             settle(e)
-        for e in (3, 4, 5, 2):
-            dispatch(e, hub_edges[e][5], hub_edges[e][4], None)
+        dispatch([(e, hub_edges[e][5], hub_edges[e][4]) for e in (3, 4, 5, 2)], None)
 
         sent = results.at[pl.ds(0, 5)]
         remote(sent, sent, result_send.at[0], result_recv.at[0], {"ka": twin}).wait_send()
@@ -612,8 +637,6 @@
     def _():
         for e, inverse, bra in outer_edges:
             offer(e, own, inverse, shift_of(bra, HALF))
-        sent_own(0, tail).wait_send()
-        pl.semaphore_signal(go, inc=1, device_id={"ka": twin}, device_id_type=mesh)
         swap(0, 2).wait_recv()
         for e in range(2):
             place_landed(e, own, e)
@@ -628,6 +651,7 @@
         for e, inverse, bra in outer_edges:
             delivered(e, HALF, bra, 2 * e)
         swap(0, 2).wait_send()
+        sent_own(0, tail).wait_send()
 
     twin_inverse = jnp.where(column % 2 == 1, 0, 1)
     twin_bra = me - column % 2
@@ -644,12 +668,16 @@
 
         @pl.when(is_inner)
         def _():
+            @pl.when(~high_source)
+            def _():
+                pl.semaphore_wait(late_in, 1)
+
             sent_own(0, tail).wait_send()
-            pl.semaphore_signal(go, inc=1, device_id={"ka": far}, device_id_type=mesh)
+            signal(go, {"ka": far})
 
         @pl.when(is_far)
         def _():
-            pl.semaphore_wait(go, 2)
+            pl.semaphore_wait(go, 1)
             send_own(third, 0, third_sems, hub)
 
         pl.when(extra_site)(extra_edge)
@@ -673,6 +701,9 @@
     @pl.when(extra_source)
     def _():
         sent_own(3).wait_send()
+
+    for n, (sends, peer) in enumerate(notices):
+        pl.when(sends)(notice(n, peer).wait_send)
 
     pltpu.make_async_copy(slots, slots, result_recv.at[0]).wait()
     found = [slots[kind, 0] + slots[kind, 1] for kind in range(ROLES)]

time: 98 us -> 96.8 us (0.988)
  Pallas kernels: 96.2 us -> 95.2 us
    pallas_call x1, Pallas kernels: 96.2 us -> 95.2 us  [meet(): pl.pallas_call(functools.partial(meet_kernel, points, slab, capacity), ou...]
where the time goes in v5:
time: 96.8 us; the launch traced here: 95.9 us
  Pallas kernels  95.2 us (98%)
    pallas_call x1, Pallas kernels, meet(): pl.pallas_call(functools.partial(meet_kernel, points, slab, capacity), ou...  95.2 us

profile of v5, /device:TPU:5, one launch (start us, length us, event | category | flops | bytes accessed | tf_op | source)
XLA Modules:
  0.0 95.9 jit_solution(1625449442378825163)
XLA Ops:
  0.0 95.2 %meet.1 = f32[3,2,32,64]{3,2,1,0:T(8,128)S(1)} custom-call(s32[1,3]{1,0:T(1,128)} %near_hbm.1, s32[1,3]{1,0:T(1,128)} %shift_hbm.1, s32[8,240]{1,0:T(8,128)} %map_hbm.1, bf16[120,2,64,128]{3,2,1,0:T(8,128)(2,1)} %bitcast.3), custom_call_target="tpu_custom_call" | custom-call | tf_op jit(solution)/shard_map/meet/pallas_call | solution.py:729
  95.2 0.6 copy.6

commit v6 on v5

--- a/solution.py
+++ b/solution.py
@@ -7,8 +7,6 @@
 from jax.experimental import pallas as pl
 from jax.experimental.pallas import tpu as pltpu
 
-EARLY = 2
-MIDDLE = 4
 ROLES = 3
 
 
@@ -180,19 +178,31 @@
     return indexes, sends, padded
 
 
-def pieces(slab):
+def cut(slab, twentieths):
     unit = slab // 20
-    sizes = [unit, 3 * unit, 4 * unit, 4 * unit, 4 * unit, 2 * unit, unit, unit - 2, 2]
-    starts = [sum(sizes[:n]) for n in range(len(sizes))]
-    return list(zip(starts, sizes))
+    sizes = [unit * n for n in twentieths]
+    return [(sum(sizes[:n]), sizes[n]) for n in range(len(sizes))]
+
+
+def main_pieces(slab):
+    return cut(slab, (1, 3, 5, 5, 4, 1, 1))
+
+
+def late_pieces(slab):
+    *most, (start, size) = cut(slab, (9, 6, 3, 1, 1))
+    return [*most, (start, size - 2), (start + size - 2, 2)]
+
+
+def extra_pieces(slab):
+    return cut(slab, (10, 6, 3, 1))
 
 
 def meet_kernel(
     points, slab, capacity, near_hbm, shift_hbm, map_hbm, own_hbm, out_ref,
     near_ref, shift_ref, map_ref, own, first, second, third, extra, packs, landed,
     meta_out, meta_in, tables, sums, results, slots, meta, table_at,
-    local_sems, meta_send, meta_recv, send_sems, first_sems, second_sems, third_sems, extra_sems,
-    swap_send, swap_recv, result_send, result_recv, go, late_in,
+    local_sems, meta_sems, send_sems, first_sems, second_sems, third_sems, extra_sems,
+    swap_send, swap_recv, result_sems, go, late_in,
 ):
     levels = 4
     row = points // levels
@@ -213,9 +223,9 @@
     lower_half = z < 2
     bands, lanes = own.shape[2], own.shape[3]
     shifts = map_hbm.shape[0]
-    parts = pieces(slab)
+    parts, late_parts, extra_parts = main_pieces(slab), late_pieces(slab), extra_pieces(slab)
     count = len(parts)
-    tail = parts[count - 2][0]
+    tail = parts[count - 1][0]
 
     barrier = pltpu.get_barrier_semaphore()
     mesh = pl.DeviceIdType.MESH
@@ -269,31 +279,29 @@
             device_id=peer, device_id_type=mesh,
         )
 
-    def chunk(c):
-        return pl.ds(*parts[c])
-
-    def send_own(target, n, sems, peer, start=0, stop=count):
-        for c in range(start, stop):
-            remote(own_hbm.at[chunk(c)], target.at[chunk(c)], send_sems.at[n], sems.at[c], {"ka": peer}).start()
+    def send_own(target, n, sems, peer, cuts):
+        for c, (start, size) in cuts:
+            part = pl.ds(start, size)
+            remote(own_hbm.at[part], target.at[part], send_sems.at[n], sems.at[c], {"ka": peer}).start()
 
     def sent_own(n, size=slab):
         part = pl.ds(0, size)
         return remote(own_hbm.at[part], own.at[part], send_sems.at[n], first_sems.at[0], {"ka": twin})
 
-    def arrived(buffer, sems, c):
-        part = buffer.at[chunk(c)]
+    def arrived(buffer, sems, c, cuts):
+        part = buffer.at[pl.ds(*cuts[c])]
         remote(part, part, send_sems.at[0], sems.at[c], {"ka": twin}).wait_recv()
 
     def main_sends(pairs):
         @pl.when(me == below)
         def _():
             for n, start, stop in pairs:
-                send_own(first, n, first_sems, hub, start, stop)
+                send_own(first, n, first_sems, hub, list(enumerate(parts))[start:stop])
 
         @pl.when(me == above)
         def _():
             for n, start, stop in pairs:
-                send_own(second, n, second_sems, hub, start, stop)
+                send_own(second, n, second_sems, hub, list(enumerate(parts))[start:stop])
 
     main_sends(((0, 0, 1),))
     near_in.wait()
@@ -321,26 +329,30 @@
         (steps_up, me + 1),
         (corner_high, row),
     )
-    heard = (
-        (is_hub, 0, 3), (is_outer, 1, 1), (me == me, 2, 1),
-        ((z >= 2) & (column % 2 == 0) & (me != 2 * row), 3, 1), (corner_low, 4, 1),
-    )
+    steps_in = (z >= 2) & (column % 2 == 0) & (me != 2 * row)
+    heard = jnp.where(is_hub, 4, jnp.where(is_outer, 2, 1)) + jnp.where(steps_in | corner_low, 1, 0)
+    told = 2 + jnp.where(steps_up | corner_high, 1, 0)
 
     def notice(n, peer):
         source = meta_out if n != 1 else meta_in.at[inner]
         target = meta_in.at[me] if n != 1 else meta_in.at[inner]
-        return remote(source, target, meta_send.at[n], meta_recv.at[n], {"ka": peer})
+        return remote(source, target, meta_sems.at[0], meta_sems.at[1], {"ka": peer})
+
+    def facts_of(amount):
+        fact = meta_in.at[pl.ds(0, amount)]
+        return remote(fact, fact, meta_sems.at[0], meta_sems.at[1], {"ka": twin})
 
     for n in (0, 2, 4):
         pl.when(notices[n][0])(notice(n, notices[n][1]).start)
 
-    main_sends(((0, 1, count - 2), (1, count - 2, count)))
+    main_sends(((0, 1, count - 1), (1, count - 1, count)))
 
     @pl.when(high_source)
     def _():
         pl.semaphore_wait(late_in, 2)
 
     pl.when(steps_up)(notice(3, me + 1).start)
+    extra_cuts = list(enumerate(extra_parts))
     extra_down = (me == 2) | (me == row + 2)
     extra_up = (me == 2 * row + 1) | (me == 2 * row + 3) | (me == 3 * row + 1)
     extra_source = extra_down | extra_up | corner_low | corner_high
@@ -352,15 +364,15 @@
 
     @pl.when(extra_down | extra_up | corner_high)
     def _():
-        send_own(extra, 3, extra_sems, extra_peer)
+        send_own(extra, 3, extra_sems, extra_peer, extra_cuts)
 
     @pl.when(corner_low)
     def _():
-        send_own(extra, 3, extra_sems, extra_peer, 0, EARLY)
+        send_own(extra, 3, extra_sems, extra_peer, extra_cuts[:1])
 
     @pl.when(is_outer | is_hub)
     def _():
-        send_own(first, 2, first_sems, twin)
+        send_own(first, 2, first_sems, twin, list(enumerate(parts)))
 
     map_in.wait()
     indexes, sends, padded = index_tables(map_ref[...], my_slice, slab, capacity)
@@ -372,15 +384,17 @@
     tables_in.start()
 
     def corner_copy(c):
-        return remote(first.at[chunk(c)], extra.at[chunk(c)], send_sems.at[5], extra_sems.at[c], {"ka": 2 * row - 1})
+        part = pl.ds(*parts[c])
+        return remote(first.at[part], extra.at[part], send_sems.at[5], extra_sems.at[0], {"ka": 2 * row - 1})
 
     def relayed(source, c):
-        return remote(source.at[chunk(c)], first.at[chunk(c)], send_sems.at[4], first_sems.at[c], {"ka": outer})
+        part = pl.ds(*parts[c])
+        return remote(source.at[part], first.at[part], send_sems.at[4], first_sems.at[c], {"ka": outer})
 
     def relay(c):
-        arrived(second, second_sems, c)
+        arrived(second, second_sems, c, parts)
         pl.when(low)(relayed(second, c).start)
-        arrived(first, first_sems, c)
+        arrived(first, first_sems, c, parts)
         pl.when(~low)(relayed(first, c).start)
         pl.when(corner_low)(corner_copy(c).start)
 
@@ -388,15 +402,10 @@
     def _():
         relay(0)
 
-    for hears, n, amount in heard:
-
-        @pl.when(hears)
-        def _():
-            fact = meta_in.at[pl.ds(0, amount)]
-            remote(fact, fact, meta_send.at[0], meta_recv.at[n], {"ka": twin}).wait_recv()
-            if n == 0:
-                notice(1, outer).start()
-
+    for amount in range(1, 6):
+        pl.when(heard == amount)(facts_of(amount).wait_recv)
+
+    pl.when(is_hub)(notice(1, outer).start)
     meta_copy = pltpu.make_async_copy(meta_in, meta, local_sems.at[1])
     meta_copy.start()
     meta_copy.wait()
@@ -413,7 +422,7 @@
     def swap(n, many=1):
         part = pl.ds(n * capacity, many * capacity)
         group = groups[n]
-        return remote(packs.at[part], landed.at[part], swap_send.at[group], swap_recv.at[group], {"ga": partner})
+        return remote(packs.at[part], landed.at[part], swap_send.at[0], swap_recv.at[group], {"ga": partner})
 
     def place_landed(n, target, place):
         def move(r, carry):
@@ -460,7 +469,7 @@
                 )
             return total
 
-        steps = [s for s in (12, 6, 4, 2) if size % s == 0][0]
+        steps = [s for s in (12, 10, 18, 6, 4, 2) if size % s == 0][0]
         if steps == size:
             sums[e] = products(start, size, sums[e])
         else:
@@ -468,17 +477,15 @@
                 0, size // steps, lambda i, total: products(start + i * steps, steps, total), sums[e]
             )
 
-    def result_copies(e, kind, bra, base):
+    def result_copies(e, kind, bra):
         copies = []
         half = bands // 2
-        for n, g in enumerate((partner, my_slice)):
+        for g in (partner, my_slice):
             source = results.at[e, pl.ds(g * half, half)]
             target = slots.at[kind, my_slice]
-            at_home = bra == me
-            near = pltpu.make_async_copy(source, target, result_recv.at[0])
-            send = 0 if base is None else base + n
-            away = remote(source, target, result_send.at[send], result_recv.at[0], {"ka": bra, "ga": g})
-            copies.append((at_home, near, away))
+            near = pltpu.make_async_copy(source, target, result_sems.at[1])
+            away = remote(source, target, result_sems.at[0], result_sems.at[1], {"ka": bra, "ga": g})
+            copies.append((bra == me, near, away))
         return copies
 
     def settle(e, inverse=None):
@@ -489,29 +496,24 @@
         left = lax.broadcasted_iota(jnp.int32, upper.shape, 1) < bands
         results[e] = upper + jnp.where(left, under, -under)
 
-    def dispatch(edges, base):
+    def dispatch(edges):
         for n in range(2):
             for e, kind, bra in edges:
-                at_home, near, away = result_copies(e, kind, bra, base)[n]
+                at_home, near, away = result_copies(e, kind, bra)[n]
                 if n == 0:
                     away.start()
                 else:
                     pl.when(at_home)(near.start)
                     pl.when(~at_home)(away.start)
 
-    def deliver(e, kind, bra, base, inverse=None):
+    def deliver(e, kind, bra, inverse=None):
         settle(e, inverse)
-        dispatch(((e, kind, bra),), base)
-
-    def delivered(e, kind, bra, base):
-        first_copy, second_copy = result_copies(e, kind, bra, base)
-        first_copy[2].wait_send()
-        pl.when(~second_copy[0])(second_copy[2].wait_send)
+        dispatch(((e, kind, bra),))
 
     sums[...] = jnp.zeros_like(sums)
     extra_inverse = jnp.where(lower_half, 1, 0)
     extra_bra = jnp.where(lower_half, me, me - 1)
-    EXTRA, EXTRA_BASE = 6, 4
+    EXTRA = 6
 
     hub_edges = (
         (first, own, 0, 0, below, ROW),
@@ -529,10 +531,10 @@
     def extra_edge():
         take(OWN_EXTRA, own, OWN_EXTRA)
         shift = shift_of(extra_bra, NEXT)
-        for c in range(count):
-            arrived(extra, extra_sems, c)
-            accumulate(EXTRA, parts[c], extra, own, OWN_EXTRA, extra_inverse, shift)
-        deliver(EXTRA, NEXT, extra_bra, EXTRA_BASE, extra_inverse)
+        for c, part in extra_cuts:
+            arrived(extra, extra_sems, c, extra_parts)
+            accumulate(EXTRA, part, extra, own, OWN_EXTRA, extra_inverse, shift)
+        deliver(EXTRA, NEXT, extra_bra, extra_inverse)
 
     @pl.when(is_hub)
     def _():
@@ -542,10 +544,6 @@
 
         for c in range(1, count):
             relay(c)
-
-        @pl.when(corner_low)
-        def _():
-            send_own(extra, 3, extra_sems, extra_peer, EARLY, MIDDLE)
 
         for n, e in ((BELOW_SLOT, 4), (ABOVE_SLOT, 5)):
             _, source, _, inverse, bra, kind = hub_edges[e]
@@ -561,11 +559,11 @@
         for e in range(2):
             still, moving, place, inverse, bra, kind = hub_edges[e]
             accumulate(e, (0, slab), still, moving, place, inverse, shift_of(bra, kind), inverse == 1)
-            deliver(e, kind, bra, None)
+            deliver(e, kind, bra)
 
         @pl.when(corner_low)
         def _():
-            send_own(extra, 3, extra_sems, extra_peer, MIDDLE, count)
+            send_own(extra, 3, extra_sems, extra_peer, extra_cuts[1:])
 
         @pl.when(extra_site)
         def _():
@@ -573,8 +571,7 @@
 
         @pl.when(corner_high)
         def _():
-            for c in range(count):
-                arrived(extra, extra_sems, c)
+            arrived(extra, extra_sems, 0, [(0, slab)])
             offer(CORNER_SLOT, extra, 0, shift_of(4 * row - 1, NEXT))
 
         swap(BELOW_SLOT, 2).wait_recv()
@@ -589,46 +586,37 @@
         def _():
             take(CORNER_SLOT, extra, 0)
 
-        for c in range(count):
-            arrived(third, third_sems, c)
-
-            @pl.when(corner_low)
-            def _():
-                arrived(extra, extra_sems, c)
-                accumulate(EXTRA, parts[c], extra, second, 1, 0, shift_of(2 * row - 1, NEXT))
-                if c == count - 1:
-                    deliver(EXTRA, NEXT, 2 * row - 1, EXTRA_BASE)
+        def late_edge(e, part):
+            still, moving, place, inverse, bra, kind = hub_edges[e]
+            accumulate(e, part, still, moving, place, inverse, shift_of(bra, kind), inverse == 1)
+
+        for c, part in enumerate(late_parts):
+            arrived(third, third_sems, c, late_parts)
+            ends = c == len(late_parts) - 1
+            for pair in ((3, 4), (5, 2)):
+                for e in pair:
+                    late_edge(e, part)
+                if ends:
+                    for e in pair:
+                        settle(e)
+                    dispatch([(e, hub_edges[e][5], hub_edges[e][4]) for e in pair])
 
             @pl.when(corner_high)
             def _():
-                accumulate(EXTRA, parts[c], third, extra, 0, 0, shift_of(4 * row - 1, NEXT))
-                if c == count - 1:
-                    deliver(EXTRA, NEXT, 4 * row - 1, EXTRA_BASE)
-
-            for e in (3, 4, 5, 2):
-                still, moving, place, inverse, bra, kind = hub_edges[e]
-                accumulate(e, parts[c], still, moving, place, inverse, shift_of(bra, kind), inverse == 1)
-
-        for e in (3, 4, 5, 2):
-            settle(e)
-        dispatch([(e, hub_edges[e][5], hub_edges[e][4]) for e in (3, 4, 5, 2)], None)
-
-        sent = results.at[pl.ds(0, 5)]
-        remote(sent, sent, result_send.at[0], result_recv.at[0], {"ka": twin}).wait_send()
-
-        @pl.when(corner_low)
-        def _():
-            delivered(EXTRA, NEXT, 2 * row - 1, EXTRA_BASE)
-            swap(CORNER_SLOT).wait_send()
-            sent_own(5).wait_send()
-
-        @pl.when(corner_high)
-        def _():
-            delivered(EXTRA, NEXT, 4 * row - 1, EXTRA_BASE)
-            swap(CORNER_SLOT).wait_send()
-
-        swap(0, 4).wait_send()
-        swap(BELOW_SLOT, 2).wait_send()
+                accumulate(EXTRA, part, third, extra, 0, 0, shift_of(4 * row - 1, NEXT))
+                if ends:
+                    deliver(EXTRA, NEXT, 4 * row - 1)
+
+            if c < len(extra_parts):
+
+                @pl.when(corner_low)
+                def _():
+                    arrived(extra, extra_sems, c, extra_parts)
+                    accumulate(EXTRA, extra_parts[c], extra, second, 1, 0, shift_of(2 * row - 1, NEXT))
+                    if c == len(extra_parts) - 1:
+                        deliver(EXTRA, NEXT, 2 * row - 1)
+
+        pl.when(corner_low)(sent_own(5).wait_send)
         sent_own(4).wait_send()
 
     outer_edges = ((0, 1, outer), (1, 0, inner))
@@ -641,16 +629,13 @@
         for e in range(2):
             place_landed(e, own, e)
         pl.when(extra_site & ~lower_half)(extra_edge)
-        for c in range(count):
-            arrived(first, first_sems, c)
+        for c, part in enumerate(parts):
+            arrived(first, first_sems, c, parts)
             for e, inverse, bra in outer_edges:
-                accumulate(e, parts[c], first, own, e, inverse, shift_of(bra, HALF), inverse == 1)
+                accumulate(e, part, first, own, e, inverse, shift_of(bra, HALF), inverse == 1)
         for e, inverse, bra in outer_edges:
-            deliver(e, HALF, bra, 2 * e)
+            deliver(e, HALF, bra)
         pl.when(extra_site & lower_half)(extra_edge)
-        for e, inverse, bra in outer_edges:
-            delivered(e, HALF, bra, 2 * e)
-        swap(0, 2).wait_send()
         sent_own(0, tail).wait_send()
 
     twin_inverse = jnp.where(column % 2 == 1, 0, 1)
@@ -662,9 +647,9 @@
         offer(0, own, twin_inverse, shift)
         take(0, own, 0)
         for c in range(count):
-            arrived(first, first_sems, c)
+            arrived(first, first_sems, c, parts)
         accumulate(0, (0, slab), first, own, 0, twin_inverse, shift)
-        deliver(0, NEXT, twin_bra, 0, twin_inverse)
+        deliver(0, NEXT, twin_bra, twin_inverse)
 
         @pl.when(is_inner)
         def _():
@@ -678,18 +663,11 @@
         @pl.when(is_far)
         def _():
             pl.semaphore_wait(go, 1)
-            send_own(third, 0, third_sems, hub)
+            send_own(third, 0, third_sems, hub, list(enumerate(late_parts)))
 
         pl.when(extra_site)(extra_edge)
-        delivered(0, NEXT, twin_bra, 0)
-        swap(0).wait_send()
         pl.when(is_far)(sent_own(0).wait_send)
 
-    @pl.when(extra_site)
-    def _():
-        delivered(EXTRA, NEXT, extra_bra, EXTRA_BASE)
-        swap(OWN_EXTRA).wait_send()
-
     @pl.when(is_outer | is_inner)
     def _():
         sent_own(1, slab - tail).wait_send()
@@ -702,10 +680,23 @@
     def _():
         sent_own(3).wait_send()
 
-    for n, (sends, peer) in enumerate(notices):
-        pl.when(sends)(notice(n, peer).wait_send)
-
-    pltpu.make_async_copy(slots, slots, result_recv.at[0]).wait()
+    for amount in (2, 3):
+        pl.when(told == amount)(facts_of(amount).wait_send)
+
+    packed = jnp.where(is_hub, 6, jnp.where(is_outer, 2, 1)) + jnp.where(extra_site | corner_low | corner_high, 1, 0)
+    for amount in (1, 2, 3, 6, 7):
+        pl.when(packed == amount)(swap(0, amount).wait_send)
+
+    own_twin = jnp.where(column % 2 == 0, 1, 2)
+    sent_results = jnp.where(is_hub, 10, jnp.where(is_outer, 3, own_twin))
+    sent_results = sent_results + jnp.where(corner_low | corner_high, 2, 0)
+    sent_results = sent_results + jnp.where(extra_site, jnp.where(lower_half, 1, 2), 0)
+    for amount in (1, 2, 3, 4, 5, 10, 12):
+        halves = results.at[pl.ds(0, amount), pl.ds(0, bands // 2)] if amount < 8 else results.at[pl.ds(0, amount // 2)]
+        done = remote(halves, halves, result_sems.at[0], result_sems.at[1], {"ka": twin})
+        pl.when(sent_results == amount)(done.wait_send)
+
+    pltpu.make_async_copy(slots, slots, result_sems.at[1]).wait()
     found = [slots[kind, 0] + slots[kind, 1] for kind in range(ROLES)]
     for b in range(ROLES):
         target = near_ref[0, b]
@@ -721,7 +712,7 @@
     shifts = block_map.shape[0]
     half = bands // 2
     dma = pltpu.SemaphoreType.DMA
-    flows = len(pieces(slab))
+    mains, lates, extras = (len(f(slab)) for f in (main_pieces, late_pieces, extra_pieces))
 
     def blocks(count):
         return pltpu.VMEM((count,) + block, own.dtype)
@@ -750,9 +741,9 @@
             pltpu.VMEM((ROLES, 2, half, 2 * bands), jnp.float32),
             pltpu.SMEM((points, 1, lanes), jnp.int32),
             pltpu.SMEM((4 * shifts, lanes), jnp.int32),
-            dma((4,)), dma((5,)), dma((5,)), dma((6,)),
-            dma((flows,)), dma((flows,)), dma((flows,)), dma((flows,)),
-            dma((4,)), dma((4,)), dma((6,)), dma((1,)),
+            dma((4,)), dma((2,)), dma((6,)),
+            dma((mains,)), dma((mains,)), dma((lates,)), dma((extras,)),
+            dma((1,)), dma((4,)), dma((2,)),
             pltpu.SemaphoreType.REGULAR,
             pltpu.SemaphoreType.REGULAR,
         ],

time: 96.8 us -> 96.1 us (level)
  Pallas kernels: 95.2 us -> 93.9 us
    pallas_call x1, Pallas kernels: 95.2 us -> 93.9 us  [meet(): pl.pallas_call(functools.partial(meet_kernel, points, slab, capacity), ou...]
where the time goes in v6:
time: 96.1 us; the launch traced here: 94.5 us
  Pallas kernels  93.9 us (98%)
    pallas_call x1, Pallas kernels, meet(): pl.pallas_call(functools.partial(meet_kernel, points, slab, capacity), ou...  93.9 us

profile of v6, /device:TPU:5, one launch (start us, length us, event | category | flops | bytes accessed | tf_op | source)
XLA Modules:
  0.0 94.5 jit_solution(17534332170707191593)
XLA Ops:
  0.0 93.9 %meet.1 = f32[3,2,32,64]{3,2,1,0:T(8,128)S(1)} custom-call(s32[1,3]{1,0:T(1,128)} %near_hbm.1, s32[1,3]{1,0:T(1,128)} %shift_hbm.1, s32[8,240]{1,0:T(8,128)} %map_hbm.1, bf16[120,2,64,128]{3,2,1,0:T(8,128)(2,1)} %bitcast.3), custom_call_target="tpu_custom_call" | custom-call | tf_op jit(solution)/shard_map/meet/pallas_call | solution.py:720
  93.9 0.6 copy.6

commit v7 on v6

--- a/solution.py
+++ b/solution.py
@@ -185,16 +185,16 @@
 
 
 def main_pieces(slab):
-    return cut(slab, (1, 3, 5, 5, 4, 1, 1))
+    return cut(slab, (1, 8, 8, 2, 1))
 
 
 def late_pieces(slab):
-    *most, (start, size) = cut(slab, (9, 6, 3, 1, 1))
+    *most, (start, size) = cut(slab, (10, 6, 3, 1))
     return [*most, (start, size - 2), (start + size - 2, 2)]
 
 
 def extra_pieces(slab):
-    return cut(slab, (10, 6, 3, 1))
+    return cut(slab, (10, 9, 1))
 
 
 def meet_kernel(

time: 96.1 us -> 96.1 us (level)
  no operation moved by 1% of the time
where the time goes in v7:
time: 96.1 us; the launch traced here: 94.4 us
  Pallas kernels  93.8 us (98%)
    pallas_call x1, Pallas kernels, meet(): pl.pallas_call(functools.partial(meet_kernel, points, slab, capacity), ou...  93.8 us

profile of v7, /device:TPU:5, one launch (start us, length us, event | category | flops | bytes accessed | tf_op | source)
XLA Modules:
  0.0 94.4 jit_solution(7466767938155478182)
XLA Ops:
  0.0 93.8 %meet.1 = f32[3,2,32,64]{3,2,1,0:T(8,128)S(1)} custom-call(s32[1,3]{1,0:T(1,128)} %near_hbm.1, s32[1,3]{1,0:T(1,128)} %shift_hbm.1, s32[8,240]{1,0:T(8,128)} %map_hbm.1, bf16[120,2,64,128]{3,2,1,0:T(8,128)(2,1)} %bitcast.3), custom_call_target="tpu_custom_call" | custom-call | tf_op jit(solution)/shard_map/meet/pallas_call | solution.py:720
  93.8 0.6 copy.6
